TPU v7x, 32 devices: a whole 2x2x4 slice. The times are simulated.
32 devices in a mesh: gx: 2 (over core), gy: 4 (over y, x), gz: 4 (over z).
Axes of the slice: x: 2, y: 2, z: 4, core: 2. Of those that a mesh axis runs over, the one named last changes fastest.
Arguments:
- right_side: float32 [3, 32, 64, 512], P(None, 'gx', 'gy', 'gz'), may hold values from -64 to 64
- damage: int32 [32, 64, 512], P('gx', 'gy', 'gz'), may hold values from 0 to 15
Outputs:
- displacement: float32 [3, 32, 64, 512], P(None, 'gx', 'gy', 'gz')
- norms: float32 [2], replicated
All inputs are finite; a program needn't handle non-finite values.
Results may differ from a plain program's by a relative error of at most 0.0003.
Values sent between devices are 32-bit elements; how exact they have to be, the bound alone decides.
A program may use at most 64 MiB of HBM per device.

v0:
```python
import functools

import jax
import jax.numpy as jnp
from jax import lax
from jax.experimental import pallas as pl
from jax.experimental.pallas import tpu as pltpu
from jax.sharding import PartitionSpec as P

BLOCK = 16
COARSE = 8
FLOOR_STIFFNESS = 0.05
MASS_TERM = 0.001
COUPLING = 2.5
RELAXATION = 0.6
DIAGONAL = 6.0 + 2.0 * COUPLING
OWN = 1.0 + COUPLING
CROSS = 0.25 * COUPLING
AXES = ("gx", "gy", "gz")
HALO = 4
LANES = 128
MESH = pl.DeviceIdType.MESH
EXACT = lax.Precision.HIGHEST


def messages():
    out = []
    for dx in (-1, 1):
        for part in range(HALO):
            out.append(("x", dx, 0, 0, part))
    for part in range(2):
        for dy in (-1, 1):
            out.append(("y", 0, dy, 0, part))
        for dx in (-1, 1):
            for dy in (-1, 1):
                if part == 1:
                    out.append(("xy", dx, dy, 0, part))
                out.append(("xyn", dx, dy, 0, part))
        if part == 0:
            for dz in (-1, 1):
                for dx in (-1, 0, 1):
                    for dy in (-1, 0, 1):
                        out.append(("z" if dx == 0 else "xz", dx, dy, dz, 0))
    return out


MESSAGES = messages()


def by_two(low, high, body, carry):
    pairs = (high - low) // 2

    def both(trip, carry):
        carry = body(low + 2 * trip, carry)
        return body(low + 2 * trip + 1, carry)

    carry = lax.fori_loop(0, pairs, both, carry)
    return body(high - 1, carry) if (high - low) % 2 else carry


def kernel(
    counts,
    extent,
    load_ref,
    damage_ref,
    out_ref,
    norms_ref,
    base,
    inverse,
    field_a,
    field_b,
    harm,
    y_send,
    y_recv,
    xy_send,
    xy_recv,
    xyn_send,
    xyn_recv,
    yz_send,
    yz_recv,
    xyz_send,
    xyz_recv,
    z_send,
    z_recv,
    xz_send,
    xz_recv,
    coarse_send,
    coarse_recv,
    coarse_w,
    spread_w,
    image_w,
    norm_send,
    norm_recv,
    local_sem,
    send_sem,
    recv_sem,
    coarse_send_sem,
    coarse_recv_sem,
    norm_send_sem,
    norm_recv_sem,
    hello_sem,
):
    count_x, count_y, count_z = counts
    ex, ey, ez = extent
    cz = ez // BLOCK
    total = count_x * count_y * count_z
    wide_x = ex + 2 * HALO
    ypad = 8
    rows = ey + 2 * ypad
    wide_y = ey + 2 * HALO
    first_y = ypad - HALO
    me = tuple(lax.axis_index(axis) for axis in AXES)
    my_id = (me[0] * count_y + me[1]) * count_z + me[2]

    def place(index):
        return (
            index // (count_y * count_z),
            lax.rem(index // count_z, count_y),
            lax.rem(index, count_z),
        )

    load_copies = []
    for x in range(ex):
        target = pl.ds((HALO + x) * rows + ypad, ey)
        load_copies.append(
            pltpu.make_async_copy(load_ref.at[:, x], base.at[0, 0:3, target], local_sem.at[x])
        )
    harm_copy = pltpu.make_async_copy(damage_ref, harm, local_sem.at[ex])
    harm_copy.start()
    for copy in load_copies:
        copy.start()

    barrier = pltpu.get_barrier_semaphore()

    reach = -(-COARSE // cz)
    window = 2 * reach + 1

    def peers(act):
        for dz in range(-reach, reach + 1):
            z = me[2] + dz

            @pl.when((z >= 0) & (z < count_z))
            def _():
                def one(step, carry):
                    if dz == 0:
                        step = step + 1
                    index = lax.rem(me[0] * count_y + me[1] + step, count_x * count_y)
                    act(index // count_y, lax.rem(index, count_y), z, dz)
                    return carry

                lax.fori_loop(0, count_x * count_y - (1 if dz == 0 else 0), one, 0)

    def greet(x, y, z, dz):
        pl.semaphore_signal(barrier, inc=1, device_id=(x, y, z), device_id_type=MESH)

    peers(greet)
    levels = jnp.minimum(me[2] + reach, count_z - 1) - jnp.maximum(me[2] - reach, 0) + 1

    harm_copy.wait()
    for x in range(ex):
        level = 1.0 - harm[x].astype(jnp.float32) / 15.0
        base[0, 3, pl.ds((HALO + x) * rows + ypad, ey)] = (
            level * level * (1.0 - FLOOR_STIFFNESS) + FLOOR_STIFFNESS
        )
    for copy in load_copies:
        copy.wait()

    lane = lax.broadcasted_iota(jnp.int32, (ey, LANES), 1)
    for side in range(2):
        for part in range(2):
            for layer in range(2):
                y = 2 * part + layer if side == 0 else ey - 2 - 2 * part + layer
                for f in range(4):
                    start = HALO * rows + ypad + y
                    for half in range(ex // 8):
                        y_send[side, part, f, layer, pl.ds(8 * half, 8)] = base[
                            0, f, pl.ds(start + 8 * half * rows, 8, stride=rows)
                        ]
                    for xs in range(2):
                        x0 = 0 if xs == 0 else ex - HALO
                        if part == 1:
                            xy_send[xs, side, f, layer] = base[
                                0, f, pl.ds(start + x0 * rows, HALO, stride=rows)
                            ]
                            continue
                        for which in range(2):
                            x0 = 2 * which if xs == 0 else ex - 2 - 2 * which
                            xyn_send[xs, side, which, f, layer] = base[
                                0, f, pl.ds(start + x0 * rows, 2, stride=rows)
                            ]
    for f in range(4):
        packed = None
        for k in range(ex):
            row = base[0, f, pl.ds((HALO + k) * rows + ypad, ey)]
            moved = pltpu.roll(row, (8 * k + HALO) % LANES, 1)
            packed = moved if packed is None else jnp.where(lane // 8 == k, moved, packed)
        z_send[f] = packed
        yz_send[0, f] = packed[:HALO]
        yz_send[1, f] = packed[ey - HALO :]
    for xs in range(2):
        packed = None
        for f in range(4):
            for j in range(HALO):
                x = j if xs == 0 else ex - HALO + j
                k = f * HALO + j
                row = base[0, f, pl.ds((HALO + x) * rows + ypad, ey)]
                moved = pltpu.roll(row, (8 * k + HALO) % LANES, 1)
                packed = moved if packed is None else jnp.where(lane // 8 == k, moved, packed)
        xz_send[xs] = packed
        xyz_send[xs, 0] = packed[:HALO]
        xyz_send[xs, 1] = packed[ey - HALO :]

    pl.semaphore_wait(barrier, levels * count_x * count_y - 1)

    def exists(dx, dy, dz):
        ok = None
        for axis, step in enumerate((dx, dy, dz)):
            if step == 0:
                continue
            here = me[axis] + step
            good = (here >= 0) & (here < counts[axis])
            ok = good if ok is None else ok & good
        return ok

    def describe(number):
        kind, dx, dy, dz, part = MESSAGES[number]
        target = (me[0] + dx, me[1] + dy, me[2] + dz)
        xs, ys, zs = (dx + 1) // 2, (dy + 1) // 2, (dz + 1) // 2
        if kind == "x":
            src_x = HALO + part if dx < 0 else ex + part
            dst_x = HALO + ex + part if dx < 0 else part
            src = base.at[0, :, pl.ds(src_x * rows + ypad, ey)]
            dst = base.at[0, :, pl.ds(dst_x * rows + ypad, ey)]
        elif kind == "y":
            src, dst = y_send.at[ys, part], y_recv.at[1 - ys, part]
        elif kind == "xy":
            src, dst = xy_send.at[xs, ys], xy_recv.at[1 - xs, 1 - ys]
        elif kind == "xyn":
            src, dst = xyn_send.at[xs, ys, part], xyn_recv.at[1 - xs, 1 - ys, part]
        else:
            own = pl.ds(ypad, ey)
            if kind == "z" and dy == 0:
                src, dst = z_send, z_recv.at[1 - zs, :, own]
            elif kind == "z":
                src, dst = yz_send.at[ys], yz_recv.at[1 - zs, 1 - ys]
            elif dy == 0:
                src, dst = xz_send.at[xs], xz_recv.at[1 - xs, 1 - zs, own]
            else:
                src, dst = xyz_send.at[xs, ys], xyz_recv.at[1 - xs, 1 - zs, 1 - ys]
        copy = pltpu.make_async_remote_copy(
            src_ref=src,
            dst_ref=dst,
            send_sem=send_sem.at[number],
            recv_sem=recv_sem.at[number],
            device_id=target,
            device_id_type=MESH,
        )
        return copy, exists(dx, dy, dz), exists(-dx, -dy, -dz)

    for number in range(len(MESSAGES)):
        copy, to_there, _ = describe(number)

        @pl.when(to_there)
        def _():
            copy.start()

    rounds = []
    radius = reach
    while radius < count_z - 1:
        rounds.append(radius)
        radius *= 2

    def hello(number):
        for side, step in enumerate((-rounds[number], rounds[number])):

            @pl.when(exists(0, 0, step))
            def _():
                pl.semaphore_signal(
                    hello_sem.at[number, 1 - side],
                    inc=1,
                    device_id=(me[0], me[1], me[2] + step),
                    device_id_type=MESH,
                )

    def hear(number):
        for side, step in enumerate((-rounds[number], rounds[number])):

            @pl.when(exists(0, 0, step))
            def _():
                pl.semaphore_wait(hello_sem.at[number, side], 1)

    if rounds:
        hello(0)

    def wait_for(part, send):
        for number, message in enumerate(MESSAGES):
            far = message[0] in ("y", "xy", "xyn") and message[4] == 1
            if send and (message[0] == "x") != (part == 0):
                continue
            if not send and far != (part == 1):
                continue
            copy, to_there, from_there = describe(number)

            @pl.when(to_there if send else from_there)
            def _():
                if send:
                    copy.wait_send()
                else:
                    copy.wait_recv()

    def unpack_y(part):
        for side in range(2):
            for layer in range(2):
                y = (
                    ypad - 2 - 2 * part + layer
                    if side == 0
                    else ypad + ey + 2 * part + layer
                )
                for f in range(4):
                    for half in range(ex // 8):
                        base[
                            0, f, pl.ds((HALO + 8 * half) * rows + y, 8, stride=rows)
                        ] = y_recv[side, part, f, layer, pl.ds(8 * half, 8)]
                    near_y = ypad - 2 + layer if side == 0 else ypad + ey + layer
                    for xs in range(2):
                        x0 = 0 if xs == 0 else HALO + ex
                        if part == 1:
                            base[0, f, pl.ds(x0 * rows + y, HALO, stride=rows)] = xy_recv[
                                xs, side, f, layer
                            ]
                        x0 = 2 - 2 * part if xs == 0 else HALO + ex + 2 * part
                        base[0, f, pl.ds(x0 * rows + near_y, 2, stride=rows)] = xyn_recv[
                            xs, side, part, f, layer
                        ]

    def unpack_z():
        lane_rows = lax.broadcasted_iota(jnp.int32, (rows, LANES), 1)
        lower = lax.rem(lane_rows, 8) < HALO
        for zs in range(2):
            for ys in range(2):
                edge = pl.ds(first_y if ys == 0 else ypad + ey, HALO)
                for f in range(4):
                    z_recv[zs, f, edge] = yz_recv[zs, ys, f]
                for xs in range(2):
                    xz_recv[xs, zs, edge] = xyz_recv[xs, zs, ys]
        for f in range(4):
            merged = jnp.where(lower, z_recv[0, f], z_recv[1, f])
            for k in range(ex):
                base[1, f, pl.ds((HALO + k) * rows, rows)] = pltpu.roll(
                    merged, (2 * LANES - 8 * k - HALO) % LANES, 1
                )
        for xs in range(2):
            merged = jnp.where(lower, xz_recv[xs, 0], xz_recv[xs, 1])
            for f in range(4):
                for j in range(HALO):
                    k = f * HALO + j
                    x = j if xs == 0 else HALO + ex + j
                    base[1, f, pl.ds(x * rows, rows)] = pltpu.roll(
                        merged, (2 * LANES - 8 * k - HALO) % LANES, 1
                    )

    lane = lax.broadcasted_iota(jnp.int32, (wide_y, LANES), 1)
    row_y = lax.broadcasted_iota(jnp.int32, (wide_y, LANES), 0)
    at_y = me[1] * ey + row_y - HALO
    good_y = (at_y >= 0) & (at_y < ey * count_y)
    good_halo = (
        good_y
        & ((me[2] > 0) | (lane < LANES // 2))
        & ((me[2] < count_z - 1) | (lane >= LANES // 2))
    )
    goods = (good_y, good_halo)

    def at(x, dy=0, own=False):
        if own:
            return pl.ds(x * rows + ypad + dy, ey)
        return pl.ds(x * rows + first_y + dy, wide_y)

    def prepare(x, carry):
        at_x = me[0] * ex + x - HALO
        good_x = (at_x >= 0) & (at_x < ex * count_x)
        for t in range(2):
            good = goods[t] & good_x
            g = jnp.where(good, base[t, 3, at(x)], 1.0)
            base[t, 3, at(x)] = g
            inv = jnp.where(good, RELAXATION / (g * DIAGONAL + MASS_TERM), 0.0)
            inverse[t, at(x)] = inv
            for c in range(3):
                load = jnp.where(good, base[t, c, at(x)], 0.0)
                base[t, c, at(x)] = load
                field_a[t, c, at(x)] = load * inv
        return carry

    def image(field, x, own=False):
        parts = [[None] * 3, [None] * 3]
        ups = [[None] * 3, [None] * 3]
        downs = [[None] * 3, [None] * 3]
        for t in range(2):

            def load(c, ox, oy):
                return field[t, c, at(x + ox, oy, own)]

            centre = [load(c, 0, 0) for c in range(3)]
            x_up = [load(c, 1, 0) for c in range(3)]
            x_down = [load(c, -1, 0) for c in range(3)]
            y_up = [load(c, 0, 1) for c in range(3)]
            y_down = [load(c, 0, -1) for c in range(3)]

            def corners(c):
                return (load(c, 1, 1) - load(c, 1, -1)) - (load(c, -1, 1) - load(c, -1, -1))

            sum_x = [x_up[c] + x_down[c] for c in range(3)]
            sum_y = [y_up[c] + y_down[c] for c in range(3)]
            parts[t][0] = DIAGONAL * centre[0] - OWN * sum_x[0] - sum_y[0] - CROSS * corners(1)
            parts[t][1] = DIAGONAL * centre[1] - sum_x[1] - OWN * sum_y[1] - CROSS * corners(0)
            parts[t][2] = DIAGONAL * centre[2] - sum_x[2] - sum_y[2]
            tilt_x = CROSS * (x_up[2] - x_down[2])
            tilt_y = CROSS * (y_up[2] - y_down[2])
            tilt_z = CROSS * ((x_up[0] - x_down[0]) + (y_up[1] - y_down[1]))
            own_z = OWN * centre[2]
            ups[t] = [centre[0] + tilt_x, centre[1] + tilt_y, own_z + tilt_z]
            downs[t] = [centre[0] - tilt_x, centre[1] - tilt_y, own_z - tilt_z]
        out = [[None] * 3, [None] * 3]
        lanes = lax.broadcasted_iota(jnp.int32, parts[0][0].shape, 1)
        first_lane = lanes == 0
        last_lane = lanes == LANES - 1
        for c in range(3):
            up = [pltpu.roll(ups[t][c], LANES - 1, 1) for t in range(2)]
            down = [pltpu.roll(downs[t][c], 1, 1) for t in range(2)]
            for t in range(2):
                beside = jnp.where(last_lane, up[1 - t], up[t]) + jnp.where(
                    first_lane, down[1 - t], down[t]
                )
                out[t][c] = parts[t][c] - beside
        return out

    def residual(field, x, tiles, own=False):
        images = image(field, x, own)
        out = []
        here = at(x, 0, own)
        for t in tiles:
            g = base[t, 3, here]
            out.append(
                [
                    base[t, c, here] - (g * images[t][c] + MASS_TERM * field[t, c, here])
                    for c in range(3)
                ]
            )
        return out

    def sweep(source, target, low, high):
        def one(x, carry):
            left = residual(source, x, (0, 1))
            for t in range(2):
                inv = inverse[t, at(x)]
                for c in range(3):
                    target[t, c, at(x)] = source[t, c, at(x)] + inv * left[t][c]
            return carry

        by_two(low, high, one, 0)

    def fold(value):
        return jnp.sum(value.reshape(ey // 8, 8, LANES), axis=0)

    zero = jnp.zeros((8, LANES), jnp.float32)

    wait_for(0, False)
    wait_for(0, True)
    unpack_y(0)
    unpack_z()
    by_two(2, wide_x - 2, prepare, 0)
    sweep(field_a, field_b, 3, wide_x - 3)

    def restrict(x, carry):
        left = residual(field_b, x, (0,), True)[0]
        sums = [carry[c] + fold(left[c]) for c in range(3)]
        sums.append(carry[3] + fold(base[0, 3, at(x, 0, True)]))
        return tuple(sums)

    sums = by_two(HALO, HALO + ex, restrict, (zero,) * 4)
    stacked = jnp.concatenate([jnp.sum(s, axis=0, keepdims=True) for s in sums] + [zero[:4]], axis=0)
    source_lane = lax.broadcasted_iota(jnp.int32, (LANES, LANES), 0)
    target_lane = lax.broadcasted_iota(jnp.int32, (LANES, LANES), 1)
    gather = (source_lane // BLOCK == lax.rem(target_lane, cz)).astype(jnp.float32)
    grouped = jnp.dot(stacked, gather, precision=EXACT, preferred_element_type=jnp.float32)
    coarse_send[...] = grouped[:4]

    def coarse_copy(x, y, z, dz):
        return pltpu.make_async_remote_copy(
            src_ref=coarse_send,
            dst_ref=coarse_recv.at[reach - dz, me[0], me[1]],
            send_sem=coarse_send_sem.at[reach + dz, x, y],
            recv_sem=coarse_recv_sem.at[reach - dz, me[0], me[1]],
            device_id=(x, y, z),
            device_id_type=MESH,
        )

    def coarse_wait(x, y, z, dz):
        pltpu.make_async_remote_copy(
            src_ref=coarse_send,
            dst_ref=coarse_recv.at[reach + dz, x, y],
            send_sem=coarse_send_sem.at[reach + dz, x, y],
            recv_sem=coarse_recv_sem.at[reach + dz, x, y],
            device_id=(x, y, z),
            device_id_type=MESH,
        ).wait()

    peers(lambda x, y, z, dz: coarse_copy(x, y, z, dz).start())
    coarse_recv[reach, me[0], me[1]] = grouped[:4]

    wait_for(1, False)
    unpack_y(1)
    by_two(0, wide_x, prepare, 0)
    sweep(field_a, field_b, 1, wide_x - 1)
    sweep(field_b, field_a, 2, wide_x - 2)

    def load_squares(x, carry):
        loads = [base[0, c, at(x, 0, True)] for c in range(3)]
        return carry + fold(sum(value * value for value in loads))

    load_sum = by_two(HALO, HALO + ex, load_squares, zero)
    wait_for(1, True)
    for number in range(len(rounds)):
        if number > 0:
            hello(number)
        hear(number)
    peers(coarse_wait)

    coarse_rows = -(-(count_y + 1) // 8) * 8
    lane_c = lax.broadcasted_iota(jnp.int32, (coarse_rows, LANES), 1)
    row_c = lax.broadcasted_iota(jnp.int32, (coarse_rows, LANES), 0)
    at_z = me[2] * cz - reach * cz + lane_c
    valid = (
        (row_c < count_y) & (at_z >= 0) & (at_z < cz * count_z) & (lane_c < window * cz)
    )
    slab = [[None] * 4 for _ in range(count_x)]
    for x in range(count_x):
        for c in range(4):
            value = None
            for w in range(window):
                column = jnp.concatenate(
                    [coarse_recv[w, x, y, c : c + 1] for y in range(count_y)]
                    + [jnp.zeros((coarse_rows - count_y, LANES), jnp.float32)],
                    axis=0,
                )
                value = column if value is None else jnp.where(lane_c // cz == w, column, value)
            slab[x][c] = jnp.where(valid, value, 0.0)
    mass = BLOCK**3 * MASS_TERM
    factor = [slab[x][3] * (BLOCK**2 / BLOCK**3) for x in range(count_x)]
    relax = [
        jnp.where(valid, RELAXATION / (factor[x] * DIAGONAL + mass), 0.0) for x in range(count_x)
    ]
    nothing = jnp.zeros((coarse_rows, LANES), jnp.float32)
    w = [[slab[x][c] * relax[x] for c in range(3)] for x in range(count_x)]

    def y_shift(value, step):
        return pltpu.roll(value, step % coarse_rows, 0)

    def z_shift(value, step):
        return pltpu.roll(value, step % LANES, 1)

    for repeat in range(COARSE - 1):
        fresh = []
        for x in range(count_x):
            here = w[x]
            above = w[x + 1] if x + 1 < count_x else [nothing] * 3
            below = w[x - 1] if x > 0 else [nothing] * 3
            sum_x = [above[c] + below[c] for c in range(3)]
            diff_x = [above[c] - below[c] for c in range(3)]
            y_up = [y_shift(here[c], -1) for c in range(3)]
            y_down = [y_shift(here[c], 1) for c in range(3)]
            sum_y = [y_up[c] + y_down[c] for c in range(3)]
            diff_y = [y_up[c] - y_down[c] for c in range(3)]
            corner_x = y_shift(diff_x[1], -1) - y_shift(diff_x[1], 1)
            corner_y = y_shift(diff_x[0], -1) - y_shift(diff_x[0], 1)
            tilt = [CROSS * diff_x[2], CROSS * diff_y[2], CROSS * (diff_x[0] + diff_y[1])]
            own = [here[0], here[1], OWN * here[2]]
            beside = [z_shift(own[c] + tilt[c], -1) + z_shift(own[c] - tilt[c], 1) for c in range(3)]
            flat = [
                DIAGONAL * here[0] - OWN * sum_x[0] - sum_y[0] - CROSS * corner_x - beside[0],
                DIAGONAL * here[1] - sum_x[1] - OWN * sum_y[1] - CROSS * corner_y - beside[1],
                DIAGONAL * here[2] - sum_x[2] - sum_y[2] - beside[2],
            ]
            fresh.append(
                [
                    here[c] + relax[x] * (slab[x][c] - (factor[x] * flat[c] + mass * here[c]))
                    for c in range(3)
                ]
            )
        w = fresh

    for x in range(count_x + 2):
        for c in range(3):
            inside = 1 <= x <= count_x
            coarse_w[x, c, pl.ds(0, 8)] = jnp.zeros((8, LANES), jnp.float32)
            coarse_w[x, c, pl.ds(8, coarse_rows)] = w[x - 1][c] if inside else nothing
    widen_core = (source_lane == reach * cz + target_lane // BLOCK).astype(jnp.float32)
    widen_halo = (
        source_lane == jnp.where(target_lane < LANES // 2, (reach + 1) * cz, reach * cz - 1)
    ).astype(jnp.float32)
    for xc in range(3):
        for c in range(3):
            cells = [coarse_w[me[0] + xc, c, pl.ds(7 + me[1] + k, 1)] for k in range(3)]
            stacked = jnp.concatenate(cells + [zero[:5]], axis=0)
            for t, matrix in enumerate((widen_core, widen_halo)):
                wide = jnp.dot(stacked, matrix, precision=EXACT, preferred_element_type=jnp.float32)
                low = jnp.broadcast_to(wide[0:1], (wide_y, LANES))
                mid = jnp.broadcast_to(wide[1:2], (wide_y, LANES))
                top = jnp.broadcast_to(wide[2:3], (wide_y, LANES))
                wide = jnp.where(row_y < HALO, low, jnp.where(row_y < HALO + ey, mid, top))
                for plane in range(3):
                    spread_w[t, c, pl.ds((3 * xc + plane) * rows + first_y, wide_y)] = wide
    for plane in range(1, 8):
        images = image(spread_w, plane)
        for t in range(2):
            for c in range(3):
                image_w[t, c, at(plane)] = images[t][c]

    def correct(x, carry):
        kind = (
            1
            + (x >= HALO - 1).astype(jnp.int32)
            + (x >= HALO).astype(jnp.int32)
            + (x >= HALO + 1).astype(jnp.int32)
            + (x >= HALO + ex - 1).astype(jnp.int32)
            + (x >= HALO + ex).astype(jnp.int32)
            + (x >= HALO + ex + 1).astype(jnp.int32)
        )
        for t in range(2):
            inv = inverse[t, at(x)]
            g = base[t, 3, at(x)]
            for c in range(3):
                added = spread_w[t, c, at(kind)]
                field_a[t, c, at(x)] = (
                    field_a[t, c, at(x)]
                    + added
                    - inv * (g * image_w[t, c, at(kind)] + MASS_TERM * added)
                )
        return carry

    by_two(2, wide_x - 2, correct, 0)
    sweep(field_a, field_b, 3, wide_x - 3)

    def squares(x, carry):
        left = residual(field_b, x, (0,), True)[0]
        for c in range(3):
            out_ref[c, x - HALO] = field_b[0, c, at(x, 0, True)]
        return carry + fold(sum(value * value for value in left))

    left_sum = by_two(HALO, HALO + ex, squares, zero)
    load_total = jnp.sum(jnp.sum(load_sum, axis=0, keepdims=True), axis=1, keepdims=True)
    left_total = jnp.sum(jnp.sum(left_sum, axis=0, keepdims=True), axis=1, keepdims=True)
    first = lax.broadcasted_iota(jnp.int32, (1, LANES), 1) == 0
    mine = jnp.where(first, load_total, left_total)
    norm_send[...] = mine

    def norm_copy(step):
        return pltpu.make_async_remote_copy(
            src_ref=norm_send,
            dst_ref=norm_recv.at[step - 1],
            send_sem=norm_send_sem.at[step - 1],
            recv_sem=norm_recv_sem.at[step - 1],
            device_id=place(lax.rem(my_id + step, total)),
            device_id_type=MESH,
        )

    def norm_start(step, carry):
        norm_copy(step).start()
        return carry

    def norm_wait(step, carry):
        norm_copy(step).wait()
        return carry

    lax.fori_loop(1, total, norm_start, 0)
    norm_recv[total - 1] = mine
    lax.fori_loop(1, total, norm_wait, 0)

    def add(device, carry):
        slot = lax.rem(my_id - device + total - 1, total)
        return carry + norm_recv[lax.rem(slot + total, total)]

    summed = lax.fori_loop(0, total, add, jnp.zeros((1, LANES), jnp.float32))
    nodes = 3 * ex * ey * ez * total
    norms_ref[...] = jnp.sqrt(summed / nodes)


def on_device(counts, right_side, damage):
    _, ex, ey, ez = right_side.shape
    cz = ez // BLOCK
    wide_x = ex + 2 * HALO
    rows = ey + 16
    flat = wide_x * rows
    wide_y = ey + 2 * HALO
    total = counts[0] * counts[1] * counts[2]
    window = 2 * (-(-COARSE // cz)) + 1
    coarse_rows = -(-(counts[1] + 1) // 8) * 8
    f32 = jnp.float32
    vmem = pltpu.VMEM
    dma = pltpu.SemaphoreType.DMA
    displacement, norms = pl.pallas_call(
        functools.partial(kernel, counts, (ex, ey, ez)),
        out_shape=(
            pltpu.VMEM(right_side.shape, f32),
            pltpu.VMEM((1, LANES), f32),
        ),
        in_specs=[pl.BlockSpec(memory_space=pl.ANY)] * 2,
        out_specs=(
            pl.BlockSpec(memory_space=pltpu.VMEM),
            pl.BlockSpec(memory_space=pltpu.VMEM),
        ),
        scratch_shapes=[
            vmem((2, 4, flat, LANES), f32),
            vmem((2, flat, LANES), f32),
            vmem((2, 3, flat, LANES), f32),
            vmem((2, 3, flat, LANES), f32),
            vmem((ex, ey, LANES), jnp.int32),
            vmem((2, 2, 4, 2, ex, LANES), f32),
            vmem((2, 2, 4, 2, ex, LANES), f32),
            vmem((2, 2, 4, 2, HALO, LANES), f32),
            vmem((2, 2, 4, 2, HALO, LANES), f32),
            vmem((2, 2, 2, 4, 2, 2, LANES), f32),
            vmem((2, 2, 2, 4, 2, 2, LANES), f32),
            vmem((2, 4, HALO, LANES), f32),
            vmem((2, 2, 4, HALO, LANES), f32),
            vmem((2, 2, HALO, LANES), f32),
            vmem((2, 2, 2, HALO, LANES), f32),
            vmem((4, ey, LANES), f32),
            vmem((2, 4, rows, LANES), f32),
            vmem((2, ey, LANES), f32),
            vmem((2, 2, rows, LANES), f32),
            vmem((4, LANES), f32),
            vmem((window, counts[0], counts[1], 4, LANES), f32),
            vmem((counts[0] + 2, 3, 8 + coarse_rows, LANES), f32),
            vmem((2, 3, 9 * rows, LANES), f32),
            vmem((2, 3, 9 * rows, LANES), f32),
            vmem((1, LANES), f32),
            vmem((total, 1, LANES), f32),
            dma((ex + 1,)),
            dma((len(MESSAGES),)),
            dma((len(MESSAGES),)),
            dma((window, counts[0], counts[1])),
            dma((window, counts[0], counts[1])),
            dma((total,)),
            dma((total,)),
            pltpu.SemaphoreType.REGULAR((8, 2)),
        ],
        compiler_params=pltpu.CompilerParams(collective_id=0, has_side_effects=True),
    )(right_side, damage)
    return displacement, norms[0, :2]


def solution(mesh):
    counts = tuple(mesh.shape[axis] for axis in AXES)
    placed = (P(None, "gx", "gy", "gz"), P("gx", "gy", "gz"))
    return jax.shard_map(
        functools.partial(on_device, counts),
        mesh=mesh,
        in_specs=placed,
        out_specs=(P(None, "gx", "gy", "gz"), P()),
        check_vma=False,
    )
```

profile of v0, /device:TPU:0, one launch (start us, length us, event | category | flops | bytes accessed | tf_op | source)
XLA Modules:
  0.0 35.4 jit_solution(12997327303901571024)
XLA Ops:
  0.6 33.5 %shard_map.41 = (f32[3,16,16,128]{3,2,1,0:T(8,128)S(1)}, f32[1,128]{1,0:T(1,128)S(1)}) custom-call(f32[3,16,16,128]{3,2,1,0:T(8,128)} %load_ref.1, s32[16,16,128]{2,1,0:T(8,128)} %damage_ref.1), custom_call_target="tpu_custom_call" | custom-call | tf_op jit(solution)/shard_map/pallas_call | solution.py:700
  34.1 0.7 %copy.5 = f32[3,16,16,128]{3,2,1,0:T(8,128)} copy(f32[3,16,16,128]{3,2,1,0:T(8,128)S(1)} %get-tuple-element.6) | data formatting | bytes 786432
  34.9 0.5 %slice_bitcast_fusion = f32[2]{0:T(128)} fusion(f32[1,128]{1,0:T(1,128)S(1)} %get-tuple-element.5), kind=kLoop, calls=%fused_computation | loop fusion | bytes 16 | tf_op jit(solution)/shard_map/squeeze | solution.py:749
where the time goes:
time: 35.5 us; the launch traced here: 35.4 us
  Pallas kernels  33.5 us (94%)
  local copies, waits for them, and re-layouts  1.26 us (4%)
  between operations  0.64 us (2%)
    pallas_call x1, Pallas kernels, on_device(): pl.pallas_call(functools.partial(kernel, counts, (ex, ey, ez)), out_shape...  33.5 us
    unnamed x1, local copies, waits for them, and re-layouts  0.75 us

commit v1 on v0

--- a/solution.py
+++ b/solution.py
@@ -487,25 +487,25 @@
     def coarse_copy(x, y, z, dz):
         return pltpu.make_async_remote_copy(
             src_ref=coarse_send,
-            dst_ref=coarse_recv.at[reach - dz, me[0], me[1]],
-            send_sem=coarse_send_sem.at[reach + dz, x, y],
-            recv_sem=coarse_recv_sem.at[reach - dz, me[0], me[1]],
+            dst_ref=coarse_recv.at[reach - dz, me[0] * count_y + me[1]],
+            send_sem=coarse_send_sem.at[reach + dz],
+            recv_sem=coarse_recv_sem.at[reach - dz],
             device_id=(x, y, z),
             device_id_type=MESH,
         )
 
-    def coarse_wait(x, y, z, dz):
-        pltpu.make_async_remote_copy(
-            src_ref=coarse_send,
-            dst_ref=coarse_recv.at[reach + dz, x, y],
-            send_sem=coarse_send_sem.at[reach + dz, x, y],
-            recv_sem=coarse_recv_sem.at[reach + dz, x, y],
-            device_id=(x, y, z),
-            device_id_type=MESH,
-        ).wait()
+    def coarse_wait():
+        for dz in range(-reach, reach + 1):
+            z = me[2] + dz
+            slots = coarse_recv.at[reach + dz, pl.ds(0, count_x * count_y - (1 if dz == 0 else 0))]
+
+            @pl.when((z >= 0) & (z < count_z))
+            def _():
+                for sem in (coarse_send_sem, coarse_recv_sem):
+                    pltpu.make_async_copy(slots, slots, sem.at[reach + dz]).wait()
 
     peers(lambda x, y, z, dz: coarse_copy(x, y, z, dz).start())
-    coarse_recv[reach, me[0], me[1]] = grouped[:4]
+    coarse_recv[reach, me[0] * count_y + me[1]] = grouped[:4]
 
     wait_for(1, False)
     unpack_y(1)
@@ -523,7 +523,7 @@
         if number > 0:
             hello(number)
         hear(number)
-    peers(coarse_wait)
+    coarse_wait()
 
     coarse_rows = -(-(count_y + 1) // 8) * 8
     lane_c = lax.broadcasted_iota(jnp.int32, (coarse_rows, LANES), 1)
@@ -538,7 +538,7 @@
             value = None
             for w in range(window):
                 column = jnp.concatenate(
-                    [coarse_recv[w, x, y, c : c + 1] for y in range(count_y)]
+                    [coarse_recv[w, x * count_y + y, c : c + 1] for y in range(count_y)]
                     + [jnp.zeros((coarse_rows - count_y, LANES), jnp.float32)],
                     axis=0,
                 )
@@ -653,33 +653,23 @@
     mine = jnp.where(first, load_total, left_total)
     norm_send[...] = mine
 
-    def norm_copy(step):
-        return pltpu.make_async_remote_copy(
+    def norm_start(step, carry):
+        pltpu.make_async_remote_copy(
             src_ref=norm_send,
-            dst_ref=norm_recv.at[step - 1],
-            send_sem=norm_send_sem.at[step - 1],
-            recv_sem=norm_recv_sem.at[step - 1],
+            dst_ref=norm_recv.at[my_id],
+            send_sem=norm_send_sem.at[0],
+            recv_sem=norm_recv_sem.at[0],
             device_id=place(lax.rem(my_id + step, total)),
             device_id_type=MESH,
-        )
-
-    def norm_start(step, carry):
-        norm_copy(step).start()
+        ).start()
         return carry
 
-    def norm_wait(step, carry):
-        norm_copy(step).wait()
-        return carry
-
     lax.fori_loop(1, total, norm_start, 0)
-    norm_recv[total - 1] = mine
-    lax.fori_loop(1, total, norm_wait, 0)
-
-    def add(device, carry):
-        slot = lax.rem(my_id - device + total - 1, total)
-        return carry + norm_recv[lax.rem(slot + total, total)]
-
-    summed = lax.fori_loop(0, total, add, jnp.zeros((1, LANES), jnp.float32))
+    norm_recv[my_id] = mine
+    others = norm_recv.at[pl.ds(0, total - 1)]
+    for sem in (norm_send_sem, norm_recv_sem):
+        pltpu.make_async_copy(others, others, sem.at[0]).wait()
+    summed = jnp.sum(norm_recv[...], axis=0)
     nodes = 3 * ex * ey * ez * total
     norms_ref[...] = jnp.sqrt(summed / nodes)
 
@@ -694,6 +684,9 @@
     total = counts[0] * counts[1] * counts[2]
     window = 2 * (-(-COARSE // cz)) + 1
     coarse_rows = -(-(counts[1] + 1) // 8) * 8
+    rounds = 0
+    while window // 2 << rounds < counts[2] - 1:
+        rounds += 1
     f32 = jnp.float32
     vmem = pltpu.VMEM
     dma = pltpu.SemaphoreType.DMA
@@ -729,7 +722,7 @@
             vmem((2, ey, LANES), f32),
             vmem((2, 2, rows, LANES), f32),
             vmem((4, LANES), f32),
-            vmem((window, counts[0], counts[1], 4, LANES), f32),
+            vmem((window, counts[0] * counts[1], 4, LANES), f32),
             vmem((counts[0] + 2, 3, 8 + coarse_rows, LANES), f32),
             vmem((2, 3, 9 * rows, LANES), f32),
             vmem((2, 3, 9 * rows, LANES), f32),
@@ -738,11 +731,11 @@
             dma((ex + 1,)),
             dma((len(MESSAGES),)),
             dma((len(MESSAGES),)),
-            dma((window, counts[0], counts[1])),
-            dma((window, counts[0], counts[1])),
-            dma((total,)),
-            dma((total,)),
-            pltpu.SemaphoreType.REGULAR((8, 2)),
+            dma((window,)),
+            dma((window,)),
+            dma((1,)),
+            dma((1,)),
+            pltpu.SemaphoreType.REGULAR((max(1, rounds), 2)),
         ],
         compiler_params=pltpu.CompilerParams(collective_id=0, has_side_effects=True),
     )(right_side, damage)

time: 35.5 us -> 33.9 us (0.955)
  Pallas kernels: 33.5 us -> 31.8 us
    pallas_call x1, Pallas kernels: 33.5 us -> 31.8 us  [on_device(): pl.pallas_call(functools.partial(kernel, counts, (ex, ey, ez)), out_shape...]
where the time goes in v1:
time: 33.9 us; the launch traced here: 33.7 us
  Pallas kernels  31.8 us (94%)
  local copies, waits for them, and re-layouts  1.26 us (4%)
  between operations  0.64 us (2%)
    pallas_call x1, Pallas kernels, on_device(): pl.pallas_call(functools.partial(kernel, counts, (ex, ey, ez)), out_shape...  31.8 us
    unnamed x1, local copies, waits for them, and re-layouts  0.75 us

profile of v1, /device:TPU:0, one launch (start us, length us, event | category | flops | bytes accessed | tf_op | source)
XLA Modules:
  0.0 33.7 jit_solution(9552308067574922832)
XLA Ops:
  0.6 31.8 %shard_map.41 = (f32[3,16,16,128]{3,2,1,0:T(8,128)S(1)}, f32[1,128]{1,0:T(1,128)S(1)}) custom-call(f32[3,16,16,128]{3,2,1,0:T(8,128)} %load_ref.1, s32[16,16,128]{2,1,0:T(8,128)} %damage_ref.1), custom_call_target="tpu_custom_call" | custom-call | tf_op jit(solution)/shard_map/pallas_call | solution.py:693
  32.5 0.7 %copy.5 = f32[3,16,16,128]{3,2,1,0:T(8,128)} copy(f32[3,16,16,128]{3,2,1,0:T(8,128)S(1)} %get-tuple-element.6) | data formatting | bytes 786432
  33.2 0.5 %slice_bitcast_fusion = f32[2]{0:T(128)} fusion(f32[1,128]{1,0:T(1,128)S(1)} %get-tuple-element.5), kind=kLoop, calls=%fused_computation | loop fusion | bytes 16 | tf_op jit(solution)/shard_map/squeeze | solution.py:742

commit v2 on v1

v2 whole, which is shorter than its diff:
```python
import functools

import jax
import jax.numpy as jnp
from jax import lax
from jax.experimental import pallas as pl
from jax.experimental.pallas import tpu as pltpu
from jax.sharding import PartitionSpec as P

BLOCK = 16
COARSE = 8
FLOOR_STIFFNESS = 0.05
MASS_TERM = 0.001
COUPLING = 2.5
RELAXATION = 0.6
KEEP = 1.0 - RELAXATION
DIAGONAL = 6.0 + 2.0 * COUPLING
OWN = 1.0 + COUPLING
CROSS = 0.25 * COUPLING
AXES = ("gx", "gy", "gz")
HALO = 4
EDGE = 2 * HALO
LANES = 128
YPAD = 8
MESH = pl.DeviceIdType.MESH
EXACT = lax.Precision.HIGHEST
NEAR = ((0, 1), (1, 1), (2, 1), (3, 1), (0, 2), (1, 2), (2, 2))
FAR = ((3, 2), (0, 3), (1, 3), (2, 3), (3, 3), (0, 4), (1, 4), (2, 4))
LAYERS = NEAR + FAR


def directions():
    out = []
    for dx in (-1, 0, 1):
        for dy in (-1, 0, 1):
            for dz in (-1, 0, 1):
                if (dx, dy, dz) != (0, 0, 0):
                    out.append((dx, dy, dz))
    return sorted(out, key=lambda d: -sum(abs(step) for step in d))


DIRECTIONS = directions()
FAR_DIRECTIONS = [d for d in DIRECTIONS if d[1] != 0]


UNROLL = 24


def by_two(low, high, body, carry):
    trips = -(-(high - low) // UNROLL)
    size = -(-(high - low) // trips)
    whole = (high - low) // size

    def several(trip, carry):
        for k in range(size):
            carry = body(low + size * trip + k, carry)
        return carry

    if whole > 1:
        carry = lax.fori_loop(0, whole, several, carry)
    else:
        carry = several(0, carry)
    for k in range(low + whole * size, high):
        carry = body(k, carry)
    return carry


def kernel(
    counts,
    extent,
    load_ref,
    damage_ref,
    out_ref,
    norms_ref,
    raw,
    stiff,
    harm,
    base,
    field_a,
    field_b,
    edge_base,
    edge_a,
    edge_b,
    sides,
    y_send,
    y_recv,
    xyn_send,
    xyn_recv,
    xy_send,
    xy_recv,
    p_all,
    q_send,
    q_all,
    py_send,
    py_recv,
    qy_send,
    qy_recv,
    coarse_send,
    coarse_recv,
    coarse_w,
    stack_w,
    spread_w,
    image_w,
    norm_send,
    norm_recv,
    amount,
    local_sem,
    send_sem,
    near_sem,
    far_sem,
    coarse_send_sem,
    coarse_recv_sem,
    norm_sem,
    hello_sem,
):
    count_x, count_y, count_z = counts
    ex, ey, ez = extent
    cz = ez // BLOCK
    total = count_x * count_y * count_z
    wide_x = ex + 2 * HALO
    ypad = YPAD
    rows = ey + 2 * ypad
    wide_y = ey + 2 * HALO
    first_y = ypad - HALO
    me = tuple(lax.axis_index(axis) for axis in AXES)
    my_id = (me[0] * count_y + me[1]) * count_z + me[2]

    def place(index):
        return (
            index // (count_y * count_z),
            lax.rem(index // count_z, count_y),
            lax.rem(index, count_z),
        )

    harm_copy = pltpu.make_async_copy(damage_ref, harm, local_sem.at[0])
    load_copy = pltpu.make_async_copy(load_ref, raw, local_sem.at[1])
    harm_copy.start()
    load_copy.start()
    barrier = pltpu.get_barrier_semaphore()

    reach = -(-COARSE // cz)
    window = 2 * reach + 1

    def peers(act):
        for dz in range(-reach, reach + 1):
            z = me[2] + dz

            @pl.when((z >= 0) & (z < count_z))
            def _():
                def one(step, carry):
                    if dz == 0:
                        step = step + 1
                    index = lax.rem(me[0] * count_y + me[1] + step, count_x * count_y)
                    act(index // count_y, lax.rem(index, count_y), z, dz)
                    return carry

                lax.fori_loop(0, count_x * count_y - (1 if dz == 0 else 0), one, 0)

    def greet(x, y, z, dz):
        pl.semaphore_signal(barrier, inc=1, device_id=(x, y, z), device_id_type=MESH)

    peers(greet)
    levels = jnp.minimum(me[2] + reach, count_z - 1) - jnp.maximum(me[2] - reach, 0) + 1

    def exists(dx, dy, dz):
        ok = None
        for axis, step in enumerate((dx, dy, dz)):
            if step == 0:
                continue
            here = me[axis] + step
            good = (here >= 0) & (here < counts[axis])
            ok = good if ok is None else ok & good
        return ok

    def block(x):
        return pl.ds((HALO + x) * rows + ypad, ey)

    for xs in range(2):

        @pl.when(jnp.logical_not(exists(2 * xs - 1, 0, 0)))
        def _():
            for part in range(HALO):
                for f in range(4):
                    x = part - HALO if xs == 0 else ex + part
                    base[f, block(x)] = jnp.zeros((ey, LANES), jnp.float32)

        for ys in range(2):

            @pl.when(jnp.logical_not(exists(2 * xs - 1, 2 * ys - 1, 0)))
            def _():
                xyn_recv[xs, ys] = jnp.zeros((len(NEAR), 2, LANES), jnp.float32)
                xy_recv[xs, ys] = jnp.zeros((len(LAYERS), HALO, LANES), jnp.float32)

    for ys in range(2):

        @pl.when(jnp.logical_not(exists(0, 2 * ys - 1, 0)))
        def _():
            y_recv[ys] = jnp.zeros((len(LAYERS), ex, LANES), jnp.float32)

    lane_own = lax.broadcasted_iota(jnp.int32, (ey, LANES), 1)
    lane = lax.broadcasted_iota(jnp.int32, (wide_y, LANES), 1)
    row_y = lax.broadcasted_iota(jnp.int32, (wide_y, LANES), 0)
    lower = lax.rem(lane, EDGE) < HALO
    at_y = me[1] * ey + row_y - HALO
    good_y = (at_y >= 0) & (at_y < ey * count_y)
    has_back, has_front = me[2] > 0, me[2] < count_z - 1
    upper_x = lax.rem(lane // (HALO * EDGE), 2) == 0
    high_z = lane >= LANES // 2
    good_x = (upper_x & (me[0] < count_x - 1)) | (~upper_x & (me[0] > 0))
    good_z = (high_z & (lower | has_front)) | (~high_z & (~lower | has_back))
    goods = (
        good_y & (~lower | has_back),
        good_y & (lower | has_front),
        good_y & good_x & good_z,
    )

    def fold(value):
        return jnp.sum(value.reshape(ey // 8, 8, LANES), axis=0)

    zero = jnp.zeros((8, LANES), jnp.float32)

    harm_copy.wait()
    load_copy.wait()

    def own_rows(x):
        return pl.ds(x * ey, ey)

    load_sum = zero
    stiff_sum = zero
    packed = [None] * 4
    for x in range(ex):
        level = 1.0 - harm[x].astype(jnp.float32) / 15.0
        g = level * level * (1.0 - FLOOR_STIFFNESS) + FLOOR_STIFFNESS
        inv = RELAXATION / (g * DIAGONAL + MASS_TERM)
        stiff[own_rows(x)] = g
        stiff_sum = stiff_sum + fold(g)
        values = []
        squared = None
        for c in range(3):
            load = raw[c, x]
            values.append(load * inv)
            squared = load * load if squared is None else squared + load * load
        load_sum = load_sum + fold(squared)
        values.append(g * inv)
        for f in range(4):
            base[f, block(x)] = values[f]
            moved = pltpu.roll(values[f], (EDGE * x + HALO) % LANES, 1)
            packed[f] = moved if x == 0 else jnp.where(lane_own // EDGE == x, moved, packed[f])
    for f in range(4):
        p_all[1, f, pl.ds(ypad, ey)] = packed[f]
        for phase in range(2):
            py_send[phase, 0, f] = packed[f][2 * phase : 2 * phase + 2]
            py_send[phase, 1, f] = packed[f][ey - 2 - 2 * phase : ey - 2 * phase]
    width = HALO * EDGE
    for xs in range(2):
        joined = None
        for f in range(4):
            shift = width * f - (0 if xs == 0 else (ex - HALO) * EDGE)
            moved = pltpu.roll(packed[f], shift % LANES, 1)
            joined = moved if f == 0 else jnp.where(lane_own // width == f, moved, joined)
        q_send[xs] = joined
        for phase in range(2):
            qy_send[phase, xs, 0] = joined[2 * phase : 2 * phase + 2]
            qy_send[phase, xs, 1] = joined[ey - 2 - 2 * phase : ey - 2 * phase]
    for side in range(2):
        for i, (f, layer) in enumerate(LAYERS):
            start = HALO * rows + ypad + (layer - 1 if side == 0 else ey - layer)
            for half in range(ex // 8):
                y_send[side, i, pl.ds(8 * half, 8)] = base[
                    f, pl.ds(start + 8 * half * rows, 8, stride=rows)
                ]
            for xs in range(2):
                x0 = 0 if xs == 0 else ex - HALO
                xy_send[xs, side, i] = base[f, pl.ds(start + x0 * rows, HALO, stride=rows)]
                if i < len(NEAR):
                    x0 = 0 if xs == 0 else ex - 2
                    xyn_send[xs, side, i] = base[f, pl.ds(start + x0 * rows, 2, stride=rows)]

    pl.semaphore_wait(barrier, levels * count_x * count_y - 1)

    def pieces(d, phase):
        dx, dy, dz = d
        xs, ys = (dx + 1) // 2, (dy + 1) // 2
        out = []
        near, far = pl.ds(0, len(NEAR)), pl.ds(len(NEAR), len(FAR))
        own = pl.ds(ypad, ey)
        if dy == 0:
            if phase == 1:
                return out
            if dz == 0:
                for part in range(HALO):
                    src_x = part if dx < 0 else ex - HALO + part
                    dst_x = ex + part if dx < 0 else part - HALO
                    out.append((base.at[:, block(src_x)], base.at[:, block(dst_x)], 4 * ey))
            if dx == 0:
                out.append((p_all.at[1, :, own], p_all.at[1 - dz, :, own], 4 * ey))
            else:
                out.append((q_send.at[xs], q_all.at[1 - xs, 1 - dz, own], ey))
            return out
        if dx == 0:
            out.append((py_send.at[phase, ys], py_recv.at[phase, 1 - ys, 1 - dz], 8))
        else:
            out.append((qy_send.at[phase, xs, ys], qy_recv.at[phase, 1 - xs, 1 - ys, 1 - dz], 2))
        if dz == 0 and dx == 0:
            part = near if phase == 0 else far
            size = len(NEAR) if phase == 0 else len(FAR)
            out.append((y_send.at[ys, part], y_recv.at[1 - ys, part], size * ex))
        elif dz == 0 and phase == 0:
            out.append((xyn_send.at[xs, ys], xyn_recv.at[1 - xs, 1 - ys], 2 * len(NEAR)))
        elif dz == 0:
            out.append((xy_send.at[xs, ys], xy_recv.at[1 - xs, 1 - ys], HALO * len(LAYERS)))
        return out

    def arrival(number, phase):
        if phase == 0:
            return near_sem.at[number]
        return far_sem.at[FAR_DIRECTIONS.index(DIRECTIONS[number])]

    def start_sends(phase):
        for number, d in enumerate(DIRECTIONS):
            parts = pieces(d, phase)
            if not parts:
                continue

            @pl.when(exists(*d))
            def _():
                for src, dst, _ in parts:
                    pltpu.make_async_remote_copy(
                        src_ref=src,
                        dst_ref=dst,
                        send_sem=send_sem.at[number],
                        recv_sem=arrival(number, phase),
                        device_id=tuple(me[axis] + d[axis] for axis in range(3)),
                        device_id_type=MESH,
                    ).start()

    start_sends(0)
    start_sends(1)

    def wait_bytes(size, sem):
        span = amount.at[pl.ds(0, size)]
        pltpu.make_async_copy(span, span, sem).wait()

    def wait_near_or_far(phase):
        for number, d in enumerate(DIRECTIONS):
            size = sum(part[2] for part in pieces(d, phase))
            if size:

                @pl.when(exists(*(-step for step in d)))
                def _():
                    wait_bytes(size, arrival(number, phase))

    def wait_sends():
        for number, d in enumerate(DIRECTIONS):
            size = sum(part[2] for phase in range(2) for part in pieces(d, phase))

            @pl.when(exists(*d))
            def _():
                wait_bytes(size, send_sem.at[number])

    rounds = []
    radius = reach
    while radius < count_z - 1:
        rounds.append(radius)
        radius *= 2

    def hello(number):
        for side, step in enumerate((-rounds[number], rounds[number])):

            @pl.when(exists(0, 0, step))
            def _():
                pl.semaphore_signal(
                    hello_sem.at[number, 1 - side],
                    inc=1,
                    device_id=(me[0], me[1], me[2] + step),
                    device_id_type=MESH,
                )

    def hear(number):
        for side, step in enumerate((-rounds[number], rounds[number])):

            @pl.when(exists(0, 0, step))
            def _():
                pl.semaphore_wait(hello_sem.at[number, side], 1)

    if rounds:
        hello(0)

    def unpack(phase):
        for side in range(2):
            for i, (f, layer) in enumerate(LAYERS):
                y = ypad - layer if side == 0 else ypad + ey + layer - 1
                if (i < len(NEAR)) == (phase == 0):
                    for half in range(ex // 8):
                        base[f, pl.ds((HALO + 8 * half) * rows + y, 8, stride=rows)] = y_recv[
                            side, i, pl.ds(8 * half, 8)
                        ]
                for xs in range(2):
                    if phase == 1:
                        x0 = 0 if xs == 0 else HALO + ex
                        base[f, pl.ds(x0 * rows + y, HALO, stride=rows)] = xy_recv[xs, side, i]
                    elif i < len(NEAR):
                        x0 = HALO - 2 if xs == 0 else HALO + ex
                        base[f, pl.ds(x0 * rows + y, 2, stride=rows)] = xyn_recv[xs, side, i]
            start = ypad - 2 - 2 * phase if side == 0 else ypad + ey + 2 * phase
            for dz in range(3):
                for f in range(4):
                    p_all[dz, f, pl.ds(start, 2)] = py_recv[phase, side, dz, f]
                for xs in range(2):
                    q_all[xs, dz, pl.ds(start, 2)] = qy_recv[phase, xs, side, dz]
        wide = pl.ds(first_y, wide_y)
        for f in range(4):
            back, here, front = (p_all[dz, f, wide] for dz in range(3))
            edge_base[f, 0, wide] = jnp.where(goods[0], jnp.where(lower, back, here), 0.0)
            edge_base[f, 1, wide] = jnp.where(goods[1], jnp.where(lower, here, front), 0.0)
        low, high = [], []
        for xs in range(2):
            back, here, front = (q_all[xs, dz, wide] for dz in range(3))
            low.append(jnp.where(lower, back, here))
            high.append(jnp.where(lower, here, front))
        for f in range(4):
            quarter = [
                pltpu.roll(value, (width * (k - f)) % LANES, 1)
                for k, value in enumerate((low[1], low[0], high[1], high[0]))
            ]
            merged = jnp.where(
                high_z,
                jnp.where(upper_x, quarter[2], quarter[3]),
                jnp.where(upper_x, quarter[0], quarter[1]),
            )
            edge_base[f, 2, wide] = jnp.where(goods[2], merged, 0.0)

    def at(p, dy=0, own=False):
        if own:
            return pl.ds(p * rows + ypad + dy, ey)
        return pl.ds(p * rows + first_y + dy, wide_y)

    cell = lane // EDGE
    last_cell = cell == LANES // EDGE - 1
    first_cell = cell == 0
    half_cell = LANES // EDGE // 2

    def turn(value, step):
        return pltpu.roll(value, step % LANES, 1)

    def edge_shift(values, step):
        low, high, outer = values
        near = [turn(value, -step * EDGE) for value in values]
        half = LANES // 2
        if step > 0:
            return [
                jnp.where(last_cell, near[2], near[0]),
                jnp.where(last_cell, turn(outer, half - EDGE), near[1]),
                jnp.where(
                    last_cell,
                    near[1],
                    jnp.where(cell == half_cell - 1, turn(low, half - EDGE), near[2]),
                ),
            ]
        return [
            jnp.where(first_cell, turn(outer, half + EDGE), near[0]),
            jnp.where(first_cell, near[2], near[1]),
            jnp.where(
                first_cell, near[0], jnp.where(cell == half_cell, turn(high, half + EDGE), near[2])
            ),
        ]

    def edge_stage(field, stage, sums=True):
        wide = pl.ds(first_y, wide_y)

        def load(c, oy):
            return [field[c, k, pl.ds(first_y + oy, wide_y)] for k in range(3)]

        centre = [load(c, 0) for c in range(3)]
        y_up = [load(c, 1) for c in range(3)]
        y_down = [load(c, -1) for c in range(3)]
        slope = [[CROSS * (y_up[c][k] - y_down[c][k]) for k in range(3)] for c in range(3)]
        used = range(3) if sums else (0, 2)
        x_up = {c: edge_shift(centre[c], 1) for c in used}
        x_down = {c: edge_shift(centre[c], -1) for c in used}
        ups, downs = [], []
        for k in range(3):
            tilt = [
                CROSS * (x_up[2][k] - x_down[2][k]),
                slope[2][k],
                CROSS * (x_up[0][k] - x_down[0][k]) + slope[1][k],
            ]
            mine = [centre[0][k], centre[1][k], OWN * centre[2][k]]
            ups.append([mine[c] + tilt[c] for c in range(3)])
            downs.append([mine[c] - tilt[c] for c in range(3)])
        front = lax.rem(lane, EDGE) == HALO
        for c in range(3):
            sides[stage, c, pl.ds(first_y, wide_y)] = jnp.where(front, ups[1][c], turn(downs[0][c], 2))
            sides[stage, c, pl.ds(rows + first_y, wide_y)] = jnp.where(
                front, turn(ups[2][c], LANES // 2), turn(downs[2][c], 2)
            )
        if not sums:
            return None
        slope_up = [edge_shift(slope[c], 1) for c in range(2)]
        slope_down = [edge_shift(slope[c], -1) for c in range(2)]
        out = []
        for k in range(3):
            sum_x = [x_up[c][k] + x_down[c][k] for c in range(3)]
            sum_y = [y_up[c][k] + y_down[c][k] for c in range(3)]
            sum_z = [turn(ups[k][c], -1) + turn(downs[k][c], 1) for c in range(3)]
            out.append(
                [
                    OWN * sum_x[0] + sum_y[0] + (slope_up[1][k] - slope_down[1][k]) + sum_z[0],
                    sum_x[1] + OWN * sum_y[1] + (slope_up[0][k] - slope_down[0][k]) + sum_z[1],
                    sum_x[2] + sum_y[2] + sum_z[2],
                ]
            )
        return out

    def edge_sweep(source, target, stage):
        beside = edge_stage(source, stage)
        wide = pl.ds(first_y, wide_y)
        for k in range(3):
            share = edge_base[3, k, wide]
            for c in range(3):
                target[c, k, wide] = (
                    KEEP * source[c, k, wide] + edge_base[c, k, wide] + share * beside[k][c]
                )

    def neighbours(field, p, x, stage, own=False):
        def load(c, ox, oy):
            return field[c, at(p + ox, oy, own)]

        if isinstance(x, int):
            ring = (x + 2 * HALO) % wide_x
            outside = ring < 2 * HALO
            where_x = ring if outside else ring - 2 * HALO
            shift = (LANES - 1 - HALO - EDGE * where_x) % LANES
            start = (rows if outside else 0) + (ypad if own else first_y)
        else:
            ring = lax.rem(x + 2 * HALO, wide_x)
            outside = ring < 2 * HALO
            where_x = jnp.where(outside, ring, ring - 2 * HALO)
            shift = lax.rem(2 * LANES - 1 - HALO - EDGE * where_x, LANES)
            start = jnp.where(outside, rows, 0) + (ypad if own else first_y)
        height = ey if own else wide_y
        centre = [load(c, 0, 0) for c in range(3)]
        x_up = [load(c, 1, 0) for c in range(3)]
        x_down = [load(c, -1, 0) for c in range(3)]
        y_up = [load(c, 0, 1) for c in range(3)]
        y_down = [load(c, 0, -1) for c in range(3)]
        slope = [CROSS * (y_up[c] - y_down[c]) for c in range(3)]
        corner = [
            CROSS * (load(c, 1, 1) - load(c, 1, -1)) - CROSS * (load(c, -1, 1) - load(c, -1, -1))
            for c in range(2)
        ]
        tilt = [
            CROSS * (x_up[2] - x_down[2]),
            slope[2],
            CROSS * (x_up[0] - x_down[0]) + slope[1],
        ]
        mine = [centre[0], centre[1], OWN * centre[2]]
        lanes = lax.broadcasted_iota(jnp.int32, (height, LANES), 1)
        sum_z = []
        for c in range(3):
            end = pltpu.roll(sides[stage, c, pl.ds(start, height)], shift, 1)
            up = jnp.where(lanes == LANES - 1, end, turn(mine[c] + tilt[c], -1))
            down = jnp.where(lanes == 0, end, turn(mine[c] - tilt[c], 1))
            sum_z.append(up + down)
        return [
            OWN * (x_up[0] + x_down[0]) + (y_up[0] + y_down[0]) + corner[1] + sum_z[0],
            (x_up[1] + x_down[1]) + OWN * (y_up[1] + y_down[1]) + corner[0] + sum_z[1],
            (x_up[2] + x_down[2]) + (y_up[2] + y_down[2]) + sum_z[2],
        ]

    def sweep(source, target, low, high, stage):
        def one(p, carry):
            beside = neighbours(source, p, p - HALO, stage)
            share = base[3, at(p)]
            for c in range(3):
                target[c, at(p)] = KEEP * source[c, at(p)] + base[c, at(p)] + share * beside[c]
            return carry

        by_two(low, high, one, 0)

    def residual(field, x, stage):
        p = x + HALO
        beside = neighbours(field, p, x, stage, True)
        g = stiff[own_rows(x)]
        heavy = g * DIAGONAL + MASS_TERM
        return [
            raw[c, x] - heavy * field[c, at(p, 0, True)] + g * beside[c] for c in range(3)
        ]

    wait_near_or_far(0)
    greeted = min(1, len(rounds) - 1)
    for number in range(greeted):
        hear(number)
        hello(number + 1)
    unpack(0)
    edge_sweep(edge_base, edge_a, 0)
    edge_stage(edge_a, 1, False)
    sweep(base, field_b, HALO - 1, HALO + ex + 1, 0)

    def restrict(x, carry):
        left = residual(field_b, x, 1)
        return tuple(carry[c] + left[c] for c in range(3))

    sums = by_two(0, ex, restrict, (jnp.zeros((ey, LANES), jnp.float32),) * 3)
    sums = [fold(s) for s in sums] + [stiff_sum]
    stacked = jnp.concatenate([jnp.sum(s, axis=0, keepdims=True) for s in sums] + [zero[:4]], axis=0)
    source_lane = lax.broadcasted_iota(jnp.int32, (LANES, LANES), 0)
    target_lane = lax.broadcasted_iota(jnp.int32, (LANES, LANES), 1)
    gather = (source_lane // BLOCK == lax.rem(target_lane, cz)).astype(jnp.float32)
    grouped = jnp.dot(stacked, gather, precision=EXACT, preferred_element_type=jnp.float32)
    coarse_send[...] = grouped[:4]

    def coarse_copy(x, y, z, dz):
        return pltpu.make_async_remote_copy(
            src_ref=coarse_send,
            dst_ref=coarse_recv.at[reach - dz, me[0] * count_y + me[1]],
            send_sem=coarse_send_sem.at[reach + dz],
            recv_sem=coarse_recv_sem.at[reach - dz],
            device_id=(x, y, z),
            device_id_type=MESH,
        )

    def coarse_wait():
        for dz in range(-reach, reach + 1):
            z = me[2] + dz
            slots = coarse_recv.at[reach + dz, pl.ds(0, count_x * count_y - (1 if dz == 0 else 0))]

            @pl.when((z >= 0) & (z < count_z))
            def _():
                for sem in (coarse_send_sem, coarse_recv_sem):
                    pltpu.make_async_copy(slots, slots, sem.at[reach + dz]).wait()

    peers(lambda x, y, z, dz: coarse_copy(x, y, z, dz).start())
    coarse_recv[reach, me[0] * count_y + me[1]] = grouped[:4]

    wait_near_or_far(1)
    unpack(1)
    edge_sweep(edge_base, edge_a, 0)
    edge_sweep(edge_a, edge_b, 1)
    sweep(base, field_a, 1, wide_x - 1, 0)
    sweep(field_a, field_b, 2, wide_x - 2, 1)
    wait_sends()
    coarse_wait()

    coarse_rows = -(-(count_y + 1) // 8) * 8
    lane_c = lax.broadcasted_iota(jnp.int32, (coarse_rows, LANES), 1)
    row_c = lax.broadcasted_iota(jnp.int32, (coarse_rows, LANES), 0)
    at_z = me[2] * cz - reach * cz + lane_c
    valid = (
        (row_c < count_y) & (at_z >= 0) & (at_z < cz * count_z) & (lane_c < window * cz)
    )
    slab = [[None] * 4 for _ in range(count_x)]
    for x in range(count_x):
        for c in range(4):
            value = None
            for w in range(window):
                column = jnp.concatenate(
                    [coarse_recv[w, x * count_y + y, c : c + 1] for y in range(count_y)]
                    + [jnp.zeros((coarse_rows - count_y, LANES), jnp.float32)],
                    axis=0,
                )
                value = column if value is None else jnp.where(lane_c // cz == w, column, value)
            slab[x][c] = jnp.where(valid, value, 0.0)
    mass = BLOCK**3 * MASS_TERM
    factor = [slab[x][3] * (BLOCK**2 / BLOCK**3) for x in range(count_x)]
    relax = [
        jnp.where(valid, RELAXATION / (factor[x] * DIAGONAL + mass), 0.0) for x in range(count_x)
    ]
    nothing = jnp.zeros((coarse_rows, LANES), jnp.float32)
    start_w = [[slab[x][c] * relax[x] for c in range(3)] for x in range(count_x)]
    share_w = [factor[x] * relax[x] for x in range(count_x)]
    w = start_w

    def y_shift(value, step):
        return pltpu.roll(value, step % coarse_rows, 0)

    for repeat in range(COARSE - 1):
        fresh = []
        for x in range(count_x):
            here = w[x]
            above = w[x + 1] if x + 1 < count_x else [nothing] * 3
            below = w[x - 1] if x > 0 else [nothing] * 3
            sum_x = [above[c] + below[c] for c in range(3)]
            diff_x = [above[c] - below[c] for c in range(3)]
            y_up = [y_shift(here[c], -1) for c in range(3)]
            y_down = [y_shift(here[c], 1) for c in range(3)]
            sum_y = [y_up[c] + y_down[c] for c in range(3)]
            diff_y = [y_up[c] - y_down[c] for c in range(3)]
            corner_x = y_shift(diff_x[1], -1) - y_shift(diff_x[1], 1)
            corner_y = y_shift(diff_x[0], -1) - y_shift(diff_x[0], 1)
            tilt = [CROSS * diff_x[2], CROSS * diff_y[2], CROSS * (diff_x[0] + diff_y[1])]
            own = [here[0], here[1], OWN * here[2]]
            sum_z = [turn(own[c] + tilt[c], -1) + turn(own[c] - tilt[c], 1) for c in range(3)]
            beside = [
                OWN * sum_x[0] + sum_y[0] + CROSS * corner_x + sum_z[0],
                sum_x[1] + OWN * sum_y[1] + CROSS * corner_y + sum_z[1],
                sum_x[2] + sum_y[2] + sum_z[2],
            ]
            fresh.append(
                [
                    KEEP * here[c] + start_w[x][c] + share_w[x] * beside[c]
                    for c in range(3)
                ]
            )
        w = fresh

    for x in range(count_x + 2):
        for c in range(3):
            inside = 1 <= x <= count_x
            coarse_w[x, c, pl.ds(0, 8)] = jnp.zeros((8, LANES), jnp.float32)
            coarse_w[x, c, pl.ds(8, coarse_rows)] = w[x - 1][c] if inside else nothing
    stack_w[pl.ds(24, 8)] = zero
    for xc in range(3):
        for c in range(3):
            stack_w[pl.ds(3 * (3 * xc + c), 3)] = coarse_w[me[0] + xc, c, pl.ds(7 + me[1], 3)]
    inner = lax.rem(target_lane, EDGE) < HALO
    first_cell_z, last_cell_z = reach * cz, (reach + 1) * cz - 1
    pick_low = jnp.where(inner, first_cell_z - 1, first_cell_z)
    pick_high = jnp.where(inner, last_cell_z, last_cell_z + 1)
    picks = (
        first_cell_z + target_lane // BLOCK,
        pick_low,
        pick_high,
        jnp.where(target_lane < LANES // 2, pick_low, pick_high),
    )
    widen = jnp.concatenate([(source_lane == pick).astype(jnp.float32) for pick in picks], axis=1)
    wide_all = jnp.dot(stack_w[...], widen, precision=EXACT, preferred_element_type=jnp.float32)

    def drawn(xc, c, k):
        parts = []
        for j in range(3):
            line = 3 * (3 * xc + c) + j
            piece = wide_all[line : line + 1, k * LANES : (k + 1) * LANES]
            parts.append(jnp.broadcast_to(piece, (wide_y, LANES)))
        return jnp.where(row_y < HALO, parts[0], jnp.where(row_y < HALO + ey, parts[1], parts[2]))

    wide = pl.ds(first_y, wide_y)
    for c in range(3):
        for xc in range(3):
            value = drawn(xc, c, 0)
            for plane in range(3):
                spread_w[c, pl.ds((3 * xc + plane) * rows + first_y, wide_y)] = value
        edge_a[c, 0, wide] = drawn(1, c, 1)
        edge_a[c, 1, wide] = drawn(1, c, 2)
        edge_a[c, 2, wide] = jnp.where(upper_x, drawn(2, c, 3), drawn(0, c, 3))
    beside = edge_stage(edge_a, 0)
    for k in range(3):
        share = edge_base[3, k, wide]
        for c in range(3):
            edge_b[c, k, wide] = (
                edge_b[c, k, wide] + KEEP * edge_a[c, k, wide] + share * beside[k][c]
            )
    edge_sweep(edge_b, edge_a, 1)
    edge_stage(edge_a, 2, False)
    for plane, x in ((1, -2), (2, -1), (3, 0), (4, ex // 2), (5, ex - 1), (6, ex), (7, ex + 1)):
        images = neighbours(spread_w, plane, x, 0)
        for c in range(3):
            image_w[c, at(plane)] = images[c]

    def correct(p, carry):
        kind = (
            jnp.int32(1)
            + jnp.int32(p >= HALO - 1)
            + jnp.int32(p >= HALO)
            + jnp.int32(p >= HALO + 1)
            + jnp.int32(p >= HALO + ex - 1)
            + jnp.int32(p >= HALO + ex)
            + jnp.int32(p >= HALO + ex + 1)
        )
        share = base[3, at(p)]
        for c in range(3):
            field_b[c, at(p)] = (
                field_b[c, at(p)] + KEEP * spread_w[c, at(kind)] + share * image_w[c, at(kind)]
            )
        return carry

    by_two(2, wide_x - 2, correct, 0)
    sweep(field_b, field_a, 3, wide_x - 3, 1)

    def squares(x, carry):
        left = residual(field_a, x, 2)
        for c in range(3):
            out_ref[c, x] = field_a[c, at(x + HALO, 0, True)]
        return carry + fold(sum(value * value for value in left))

    left_sum = by_two(0, ex, squares, zero)
    load_total = jnp.sum(jnp.sum(load_sum, axis=0, keepdims=True), axis=1, keepdims=True)
    left_total = jnp.sum(jnp.sum(left_sum, axis=0, keepdims=True), axis=1, keepdims=True)
    first = lax.broadcasted_iota(jnp.int32, (1, LANES), 1) == 0
    mine = jnp.where(first, load_total, left_total)
    norm_send[...] = mine

    def norm_start(step, carry):
        pltpu.make_async_remote_copy(
            src_ref=norm_send,
            dst_ref=norm_recv.at[my_id],
            send_sem=norm_sem.at[0],
            recv_sem=norm_sem.at[1],
            device_id=place(lax.rem(my_id + step, total)),
            device_id_type=MESH,
        ).start()
        return carry

    for number in range(greeted, len(rounds)):
        if number > greeted:
            hello(number)
        hear(number)
    lax.fori_loop(1, total, norm_start, 0)
    norm_recv[my_id] = mine
    others = norm_recv.at[pl.ds(0, total - 1)]
    for k in range(2):
        pltpu.make_async_copy(others, others, norm_sem.at[k]).wait()
    summed = jnp.sum(norm_recv[...], axis=0)
    nodes = 3 * ex * ey * ez * total
    norms_ref[...] = jnp.sqrt(summed / nodes)


def on_device(counts, right_side, damage):
    _, ex, ey, ez = right_side.shape
    assert ez == LANES and ex * EDGE == LANES and 2 * EDGE * EDGE == LANES
    assert ex % BLOCK == 0 and ey == BLOCK and ex == BLOCK
    cz = ez // BLOCK
    wide_x = ex + 2 * HALO
    rows = ey + 2 * YPAD
    flat = wide_x * rows
    total = counts[0] * counts[1] * counts[2]
    window = 2 * (-(-COARSE // cz)) + 1
    coarse_rows = -(-(counts[1] + 1) // 8) * 8
    rounds = 0
    while window // 2 << rounds < counts[2] - 1:
        rounds += 1
    f32 = jnp.float32

    def vmem(*shape):
        return pltpu.VMEM(shape + (LANES,), f32)

    dma = pltpu.SemaphoreType.DMA
    near, layers = len(NEAR), len(LAYERS)
    displacement, norms = pl.pallas_call(
        functools.partial(kernel, counts, (ex, ey, ez)),
        out_shape=(
            pltpu.VMEM(right_side.shape, f32),
            pltpu.VMEM((1, LANES), f32),
        ),
        in_specs=[pl.BlockSpec(memory_space=pl.ANY)] * 2,
        out_specs=(
            pl.BlockSpec(memory_space=pltpu.VMEM),
            pl.BlockSpec(memory_space=pltpu.VMEM),
        ),
        scratch_shapes=[
            vmem(3, ex, ey),
            vmem(ex * ey),
            pltpu.VMEM((ex, ey, LANES), jnp.int32),
            vmem(4, flat),
            vmem(3, flat),
            vmem(3, flat),
            vmem(4, 3, rows),
            vmem(3, 3, rows),
            vmem(3, 3, rows),
            vmem(3, 3, 2 * rows),
            vmem(2, layers, ex),
            vmem(2, layers, ex),
            vmem(2, 2, near, 2),
            vmem(2, 2, near, 2),
            vmem(2, 2, layers, HALO),
            vmem(2, 2, layers, HALO),
            vmem(3, 4, rows),
            vmem(2, ey),
            vmem(2, 3, rows),
            vmem(2, 2, 4, 2),
            vmem(2, 2, 3, 4, 2),
            vmem(2, 2, 2, 2),
            vmem(2, 2, 2, 3, 2),
            vmem(4),
            vmem(window, counts[0] * counts[1], 4),
            vmem(counts[0] + 2, 3, 8 + coarse_rows),
            vmem(32),
            vmem(3, 9 * rows),
            vmem(3, 9 * rows),
            vmem(1),
            vmem(total, 1),
            vmem(4 * HALO * ey + ey, 1),
            dma((2,)),
            dma((len(DIRECTIONS),)),
            dma((len(DIRECTIONS),)),
            dma((len(FAR_DIRECTIONS),)),
            dma((window,)),
            dma((window,)),
            dma((2,)),
            pltpu.SemaphoreType.REGULAR((max(1, rounds), 2)),
        ],
        compiler_params=pltpu.CompilerParams(collective_id=0, has_side_effects=True),
    )(right_side, damage)
    return displacement, norms[0, :2]


def solution(mesh):
    counts = tuple(mesh.shape[axis] for axis in AXES)
    placed = (P(None, "gx", "gy", "gz"), P("gx", "gy", "gz"))
    return jax.shard_map(
        functools.partial(on_device, counts),
        mesh=mesh,
        in_specs=placed,
        out_specs=(P(None, "gx", "gy", "gz"), P()),
        check_vma=False,
    )
```

time: 33.9 us -> 28.7 us (0.85)
  Pallas kernels: 31.8 us -> 26.6 us
    pallas_call x1, Pallas kernels: 31.8 us -> 26.6 us  [on_device(): pl.pallas_call(functools.partial(kernel, counts, (ex, ey, ez)), out_shape...]
where the time goes in v2:
time: 28.7 us; the launch traced here: 28.5 us
  Pallas kernels  26.6 us (93%)
  local copies, waits for them, and re-layouts  1.26 us (4%)
  between operations  0.64 us (2%)
    pallas_call x1, Pallas kernels, on_device(): pl.pallas_call(functools.partial(kernel, counts, (ex, ey, ez)), out_shape...  26.6 us
    unnamed x1, local copies, waits for them, and re-layouts  0.75 us

profile of v2, /device:TPU:0, one launch (start us, length us, event | category | flops | bytes accessed | tf_op | source)
XLA Modules:
  0.0 28.5 jit_solution(13300399303382061159)
XLA Ops:
  0.6 26.6 %shard_map.41 = (f32[3,16,16,128]{3,2,1,0:T(8,128)S(1)}, f32[1,128]{1,0:T(1,128)S(1)}) custom-call(f32[3,16,16,128]{3,2,1,0:T(8,128)} %load_ref.1, s32[16,16,128]{2,1,0:T(8,128)} %damage_ref.1), custom_call_target="tpu_custom_call" | custom-call | tf_op jit(solution)/shard_map/pallas_call | solution.py:839
  27.3 0.7 %copy.5 = f32[3,16,16,128]{3,2,1,0:T(8,128)} copy(f32[3,16,16,128]{3,2,1,0:T(8,128)S(1)} %get-tuple-element.6) | data formatting | bytes 786432
  28.0 0.5 %slice_bitcast_fusion = f32[2]{0:T(128)} fusion(f32[1,128]{1,0:T(1,128)S(1)} %get-tuple-element.5), kind=kLoop, calls=%fused_computation | loop fusion | bytes 16 | tf_op jit(solution)/shard_map/squeeze | solution.py:894

commit v3 on v2

--- a/solution.py
+++ b/solution.py
@@ -40,7 +40,6 @@
 
 
 DIRECTIONS = directions()
-FAR_DIRECTIONS = [d for d in DIRECTIONS if d[1] != 0]
 
 
 UNROLL = 24
@@ -105,11 +104,8 @@
     norm_recv,
     amount,
     local_sem,
-    send_sem,
-    near_sem,
-    far_sem,
-    coarse_send_sem,
-    coarse_recv_sem,
+    halo_sem,
+    coarse_sem,
     norm_sem,
     hello_sem,
 ):
@@ -141,20 +137,25 @@
     reach = -(-COARSE // cz)
     window = 2 * reach + 1
 
+    def around(here, count):
+        out = [here]
+        for step in range(1, count):
+            there = here + step
+            out.append(jnp.where(there >= count, there - count, there))
+        return out
+
+    ring_x, ring_y, ring_z = (around(me[axis], counts[axis]) for axis in range(3))
+
     def peers(act):
-        for dz in range(-reach, reach + 1):
+        for dz in sorted(range(-reach, reach + 1), key=lambda step: -abs(step)):
             z = me[2] + dz
 
             @pl.when((z >= 0) & (z < count_z))
             def _():
-                def one(step, carry):
-                    if dz == 0:
-                        step = step + 1
-                    index = lax.rem(me[0] * count_y + me[1] + step, count_x * count_y)
-                    act(index // count_y, lax.rem(index, count_y), z, dz)
-                    return carry
-
-                lax.fori_loop(0, count_x * count_y - (1 if dz == 0 else 0), one, 0)
+                for x in reversed(ring_x):
+                    for y in reversed(ring_y):
+                        if dz != 0 or x is not me[0] or y is not me[1]:
+                            act(x, y, z, dz)
 
     def greet(x, y, z, dz):
         pl.semaphore_signal(barrier, inc=1, device_id=(x, y, z), device_id_type=MESH)
@@ -311,25 +312,27 @@
             out.append((xy_send.at[xs, ys], xy_recv.at[1 - xs, 1 - ys], HALO * len(LAYERS)))
         return out
 
-    def arrival(number, phase):
-        if phase == 0:
-            return near_sem.at[number]
-        return far_sem.at[FAR_DIRECTIONS.index(DIRECTIONS[number])]
-
     def start_sends(phase):
-        for number, d in enumerate(DIRECTIONS):
+        odd = lax.rem(me[1], 2) == 1
+        ordered = []
+        for turn_number in range(2):
+            for number, d in enumerate(DIRECTIONS):
+                if d[1] != 0:
+                    ordered.append((number, d, odd == ((d[1] > 0) == (turn_number == 0))))
+        ordered += [(number, d, None) for number, d in enumerate(DIRECTIONS) if d[1] == 0]
+        for number, d, condition in ordered:
             parts = pieces(d, phase)
             if not parts:
                 continue
 
-            @pl.when(exists(*d))
+            @pl.when(exists(*d) if condition is None else exists(*d) & condition)
             def _():
                 for src, dst, _ in parts:
                     pltpu.make_async_remote_copy(
                         src_ref=src,
                         dst_ref=dst,
-                        send_sem=send_sem.at[number],
-                        recv_sem=arrival(number, phase),
+                        send_sem=halo_sem.at[2],
+                        recv_sem=halo_sem.at[phase],
                         device_id=tuple(me[axis] + d[axis] for axis in range(3)),
                         device_id_type=MESH,
                     ).start()
@@ -341,22 +344,33 @@
         span = amount.at[pl.ds(0, size)]
         pltpu.make_async_copy(span, span, sem).wait()
 
-    def wait_near_or_far(phase):
-        for number, d in enumerate(DIRECTIONS):
-            size = sum(part[2] for part in pieces(d, phase))
-            if size:
-
-                @pl.when(exists(*(-step for step in d)))
-                def _():
-                    wait_bytes(size, arrival(number, phase))
-
-    def wait_sends():
-        for number, d in enumerate(DIRECTIONS):
-            size = sum(part[2] for phase in range(2) for part in pieces(d, phase))
-
-            @pl.when(exists(*d))
-            def _():
-                wait_bytes(size, send_sem.at[number])
+    sides_of = [
+        (here > 0).astype(jnp.int32) + (here < count - 1).astype(jnp.int32)
+        for here, count in zip(me, counts)
+    ]
+    most = [min(2, count - 1) for count in counts]
+
+    def wait_halo(phases, sem):
+        for number_x in range(min(1, most[0]), most[0] + 1):
+            for number_y in range(min(1, most[1]), most[1] + 1):
+                for number_z in range(min(1, most[2]), most[2] + 1):
+                    have = (number_x, number_y, number_z)
+                    size = 0
+                    for d in DIRECTIONS:
+                        if d == tuple(-abs(step) for step in d):
+                            times = 1
+                            for step, number in zip(d, have):
+                                times *= number if step else 1
+                            for phase in phases:
+                                size += times * sum(part[2] for part in pieces(d, phase))
+
+                    @pl.when(
+                        (sides_of[0] == number_x)
+                        & (sides_of[1] == number_y)
+                        & (sides_of[2] == number_z)
+                    )
+                    def _():
+                        wait_bytes(size, sem)
 
     rounds = []
     radius = reach
@@ -587,7 +601,7 @@
             raw[c, x] - heavy * field[c, at(p, 0, True)] + g * beside[c] for c in range(3)
         ]
 
-    wait_near_or_far(0)
+    wait_halo((0,), halo_sem.at[0])
     greeted = min(1, len(rounds) - 1)
     for number in range(greeted):
         hear(number)
@@ -614,32 +628,30 @@
         return pltpu.make_async_remote_copy(
             src_ref=coarse_send,
             dst_ref=coarse_recv.at[reach - dz, me[0] * count_y + me[1]],
-            send_sem=coarse_send_sem.at[reach + dz],
-            recv_sem=coarse_recv_sem.at[reach - dz],
+            send_sem=coarse_sem.at[0],
+            recv_sem=coarse_sem.at[1],
             device_id=(x, y, z),
             device_id_type=MESH,
         )
 
     def coarse_wait():
-        for dz in range(-reach, reach + 1):
-            z = me[2] + dz
-            slots = coarse_recv.at[reach + dz, pl.ds(0, count_x * count_y - (1 if dz == 0 else 0))]
-
-            @pl.when((z >= 0) & (z < count_z))
+        for number in range(1, window + 1):
+
+            @pl.when(levels == number)
             def _():
-                for sem in (coarse_send_sem, coarse_recv_sem):
-                    pltpu.make_async_copy(slots, slots, sem.at[reach + dz]).wait()
+                for k in range(2):
+                    wait_bytes(4 * (number * count_x * count_y - 1), coarse_sem.at[k])
 
     peers(lambda x, y, z, dz: coarse_copy(x, y, z, dz).start())
     coarse_recv[reach, me[0] * count_y + me[1]] = grouped[:4]
 
-    wait_near_or_far(1)
+    wait_halo((1,), halo_sem.at[1])
     unpack(1)
     edge_sweep(edge_base, edge_a, 0)
     edge_sweep(edge_a, edge_b, 1)
     sweep(base, field_a, 1, wide_x - 1, 0)
     sweep(field_a, field_b, 2, wide_x - 2, 1)
-    wait_sends()
+    wait_halo((0, 1), halo_sem.at[2])
     coarse_wait()
 
     coarse_rows = -(-(count_y + 1) // 8) * 8
@@ -790,22 +802,22 @@
     mine = jnp.where(first, load_total, left_total)
     norm_send[...] = mine
 
-    def norm_start(step, carry):
-        pltpu.make_async_remote_copy(
-            src_ref=norm_send,
-            dst_ref=norm_recv.at[my_id],
-            send_sem=norm_sem.at[0],
-            recv_sem=norm_sem.at[1],
-            device_id=place(lax.rem(my_id + step, total)),
-            device_id_type=MESH,
-        ).start()
-        return carry
-
     for number in range(greeted, len(rounds)):
         if number > greeted:
             hello(number)
         hear(number)
-    lax.fori_loop(1, total, norm_start, 0)
+    for x in reversed(ring_x):
+        for z in reversed(ring_z):
+            for y in reversed(ring_y):
+                if x is not me[0] or y is not me[1] or z is not me[2]:
+                    pltpu.make_async_remote_copy(
+                        src_ref=norm_send,
+                        dst_ref=norm_recv.at[my_id],
+                        send_sem=norm_sem.at[0],
+                        recv_sem=norm_sem.at[1],
+                        device_id=(x, y, z),
+                        device_id_type=MESH,
+                    ).start()
     norm_recv[my_id] = mine
     others = norm_recv.at[pl.ds(0, total - 1)]
     for k in range(2):
@@ -879,13 +891,10 @@
             vmem(3, 9 * rows),
             vmem(1),
             vmem(total, 1),
-            vmem(4 * HALO * ey + ey, 1),
+            vmem(4 * EDGE * LANES, 1),
             dma((2,)),
-            dma((len(DIRECTIONS),)),
-            dma((len(DIRECTIONS),)),
-            dma((len(FAR_DIRECTIONS),)),
-            dma((window,)),
-            dma((window,)),
+            dma((3,)),
+            dma((2,)),
             dma((2,)),
             pltpu.SemaphoreType.REGULAR((max(1, rounds), 2)),
         ],

time: 28.7 us -> 27.4 us (0.955)
  Pallas kernels: 26.6 us -> 25.4 us
    pallas_call x1, Pallas kernels: 26.6 us -> 25.4 us  [on_device(): pl.pallas_call(functools.partial(kernel, counts, (ex, ey, ez)), out_shape...]
where the time goes in v3:
time: 27.4 us; the launch traced here: 27.3 us
  Pallas kernels  25.4 us (93%)
  local copies, waits for them, and re-layouts  1.26 us (5%)
  between operations  0.64 us (2%)
    pallas_call x1, Pallas kernels, on_device(): pl.pallas_call(functools.partial(kernel, counts, (ex, ey, ez)), out_shape...  25.4 us
    unnamed x1, local copies, waits for them, and re-layouts  0.75 us

profile of v3, /device:TPU:0, one launch (start us, length us, event | category | flops | bytes accessed | tf_op | source)
XLA Modules:
  0.0 27.3 jit_solution(7129659042070200719)
XLA Ops:
  0.6 25.4 %shard_map.41 = (f32[3,16,16,128]{3,2,1,0:T(8,128)S(1)}, f32[1,128]{1,0:T(1,128)S(1)}) custom-call(f32[3,16,16,128]{3,2,1,0:T(8,128)} %load_ref.1, s32[16,16,128]{2,1,0:T(8,128)} %damage_ref.1), custom_call_target="tpu_custom_call" | custom-call | tf_op jit(solution)/shard_map/pallas_call | solution.py:851
  26.0 0.7 %copy.5 = f32[3,16,16,128]{3,2,1,0:T(8,128)} copy(f32[3,16,16,128]{3,2,1,0:T(8,128)S(1)} %get-tuple-element.6) | data formatting | bytes 786432
  26.7 0.5 %slice_bitcast_fusion = f32[2]{0:T(128)} fusion(f32[1,128]{1,0:T(1,128)S(1)} %get-tuple-element.5), kind=kLoop, calls=%fused_computation | loop fusion | bytes 16 | tf_op jit(solution)/shard_map/squeeze | solution.py:903

commit v4 on v3

--- a/solution.py
+++ b/solution.py
@@ -81,6 +81,7 @@
     edge_a,
     edge_b,
     sides,
+    swung,
     y_send,
     y_recv,
     xyn_send,
@@ -285,28 +286,30 @@
         out = []
         near, far = pl.ds(0, len(NEAR)), pl.ds(len(NEAR), len(FAR))
         own = pl.ds(ypad, ey)
+        edges, late = phase % 2 == 0, phase // 2
         if dy == 0:
-            if phase == 1:
+            if late:
                 return out
-            if dz == 0:
+            if dz == 0 and not edges:
                 for part in range(HALO):
                     src_x = part if dx < 0 else ex - HALO + part
                     dst_x = ex + part if dx < 0 else part - HALO
                     out.append((base.at[:, block(src_x)], base.at[:, block(dst_x)], 4 * ey))
-            if dx == 0:
+            if dx == 0 and edges:
                 out.append((p_all.at[1, :, own], p_all.at[1 - dz, :, own], 4 * ey))
-            else:
+            elif edges:
                 out.append((q_send.at[xs], q_all.at[1 - xs, 1 - dz, own], ey))
             return out
-        if dx == 0:
-            out.append((py_send.at[phase, ys], py_recv.at[phase, 1 - ys, 1 - dz], 8))
-        else:
-            out.append((qy_send.at[phase, xs, ys], qy_recv.at[phase, 1 - xs, 1 - ys, 1 - dz], 2))
-        if dz == 0 and dx == 0:
-            part = near if phase == 0 else far
-            size = len(NEAR) if phase == 0 else len(FAR)
+        if edges:
+            if dx == 0:
+                out.append((py_send.at[late, ys], py_recv.at[late, 1 - ys, 1 - dz], 8))
+            else:
+                out.append((qy_send.at[late, xs, ys], qy_recv.at[late, 1 - xs, 1 - ys, 1 - dz], 2))
+        elif dz == 0 and dx == 0:
+            part = far if late else near
+            size = len(FAR) if late else len(NEAR)
             out.append((y_send.at[ys, part], y_recv.at[1 - ys, part], size * ex))
-        elif dz == 0 and phase == 0:
+        elif dz == 0 and not late:
             out.append((xyn_send.at[xs, ys], xyn_recv.at[1 - xs, 1 - ys], 2 * len(NEAR)))
         elif dz == 0:
             out.append((xy_send.at[xs, ys], xy_recv.at[1 - xs, 1 - ys], HALO * len(LAYERS)))
@@ -331,14 +334,14 @@
                     pltpu.make_async_remote_copy(
                         src_ref=src,
                         dst_ref=dst,
-                        send_sem=halo_sem.at[2],
+                        send_sem=halo_sem.at[4],
                         recv_sem=halo_sem.at[phase],
                         device_id=tuple(me[axis] + d[axis] for axis in range(3)),
                         device_id_type=MESH,
                     ).start()
 
-    start_sends(0)
-    start_sends(1)
+    for phase in range(4):
+        start_sends(phase)
 
     def wait_bytes(size, sem):
         span = amount.at[pl.ds(0, size)]
@@ -400,7 +403,7 @@
     if rounds:
         hello(0)
 
-    def unpack(phase):
+    def unpack_main(phase):
         for side in range(2):
             for i, (f, layer) in enumerate(LAYERS):
                 y = ypad - layer if side == 0 else ypad + ey + layer - 1
@@ -416,6 +419,9 @@
                     elif i < len(NEAR):
                         x0 = HALO - 2 if xs == 0 else HALO + ex
                         base[f, pl.ds(x0 * rows + y, 2, stride=rows)] = xyn_recv[xs, side, i]
+
+    def unpack_edges(phase):
+        for side in range(2):
             start = ypad - 2 - 2 * phase if side == 0 else ypad + ey + 2 * phase
             for dz in range(3):
                 for f in range(4):
@@ -449,6 +455,26 @@
             return pl.ds(p * rows + ypad + dy, ey)
         return pl.ds(p * rows + first_y + dy, wide_y)
 
+    outer = lax.broadcasted_iota(jnp.int32, (EDGE, LANES), 0) < HALO
+
+    def take(ref, index, start, dy, mode):
+        if mode == "wide":
+            return ref[index + (pl.ds(start + first_y + dy, wide_y),)]
+        if mode == "own":
+            return ref[index + (pl.ds(start + ypad + dy, ey),)]
+        low = ref[index + (pl.ds(start + first_y + dy, EDGE),)]
+        high = ref[index + (pl.ds(start + ypad + ey - HALO + dy, EDGE),)]
+        return jnp.where(outer, low, high)
+
+    def put(ref, index, start, mode, value):
+        if mode == "wide":
+            ref[index + (pl.ds(start + first_y, wide_y),)] = value
+        elif mode == "own":
+            ref[index + (pl.ds(start + ypad, ey),)] = value
+        else:
+            ref[index + (pl.ds(start + first_y, HALO),)] = value[:HALO]
+            ref[index + (pl.ds(start + ypad + ey, HALO),)] = value[HALO:]
+
     cell = lane // EDGE
     last_cell = cell == LANES // EDGE - 1
     first_cell = cell == 0
@@ -462,21 +488,17 @@
         near = [turn(value, -step * EDGE) for value in values]
         half = LANES // 2
         if step > 0:
+            far = turn(jnp.where(cell == half_cell, outer, low), half - EDGE)
             return [
                 jnp.where(last_cell, near[2], near[0]),
-                jnp.where(last_cell, turn(outer, half - EDGE), near[1]),
-                jnp.where(
-                    last_cell,
-                    near[1],
-                    jnp.where(cell == half_cell - 1, turn(low, half - EDGE), near[2]),
-                ),
+                jnp.where(last_cell, far, near[1]),
+                jnp.where(last_cell, near[1], jnp.where(cell == half_cell - 1, far, near[2])),
             ]
+        far = turn(jnp.where(cell == half_cell - 1, outer, high), half + EDGE)
         return [
-            jnp.where(first_cell, turn(outer, half + EDGE), near[0]),
+            jnp.where(first_cell, far, near[0]),
             jnp.where(first_cell, near[2], near[1]),
-            jnp.where(
-                first_cell, near[0], jnp.where(cell == half_cell, turn(high, half + EDGE), near[2])
-            ),
+            jnp.where(first_cell, near[0], jnp.where(cell == half_cell, far, near[2])),
         ]
 
     def edge_stage(field, stage, sums=True):
@@ -510,8 +532,22 @@
             )
         if not sums:
             return None
-        slope_up = [edge_shift(slope[c], 1) for c in range(2)]
-        slope_down = [edge_shift(slope[c], -1) for c in range(2)]
+        slope_up, slope_down = [], []
+        for c in range(2):
+            for shifted, out in ((x_up, slope_up), (x_down, slope_down)):
+                slot = 2 * c + (0 if out is slope_up else 1)
+                for k in range(3):
+                    swung[slot, k, wide] = shifted[c][k]
+                out.append(
+                    [
+                        CROSS
+                        * (
+                            swung[slot, k, pl.ds(first_y + 1, wide_y)]
+                            - swung[slot, k, pl.ds(first_y - 1, wide_y)]
+                        )
+                        for k in range(3)
+                    ]
+                )
         out = []
         for k in range(3):
             sum_x = [x_up[c][k] + x_down[c][k] for c in range(3)]
@@ -536,23 +572,14 @@
                     KEEP * source[c, k, wide] + edge_base[c, k, wide] + share * beside[k][c]
                 )
 
-    def neighbours(field, p, x, stage, own=False):
+    def neighbours(field, p, x, stage, mode="wide"):
         def load(c, ox, oy):
-            return field[c, at(p + ox, oy, own)]
-
-        if isinstance(x, int):
-            ring = (x + 2 * HALO) % wide_x
-            outside = ring < 2 * HALO
-            where_x = ring if outside else ring - 2 * HALO
-            shift = (LANES - 1 - HALO - EDGE * where_x) % LANES
-            start = (rows if outside else 0) + (ypad if own else first_y)
-        else:
-            ring = lax.rem(x + 2 * HALO, wide_x)
-            outside = ring < 2 * HALO
-            where_x = jnp.where(outside, ring, ring - 2 * HALO)
-            shift = lax.rem(2 * LANES - 1 - HALO - EDGE * where_x, LANES)
-            start = jnp.where(outside, rows, 0) + (ypad if own else first_y)
-        height = ey if own else wide_y
+            return take(field, (c,), (p + ox) * rows, oy, mode)
+
+        ring = (x + 2 * HALO) % wide_x
+        outside = ring < 2 * HALO
+        where_x = ring if outside else ring - 2 * HALO
+        shift = (LANES - 1 - HALO - EDGE * where_x) % LANES
         centre = [load(c, 0, 0) for c in range(3)]
         x_up = [load(c, 1, 0) for c in range(3)]
         x_down = [load(c, -1, 0) for c in range(3)]
@@ -569,10 +596,10 @@
             CROSS * (x_up[0] - x_down[0]) + slope[1],
         ]
         mine = [centre[0], centre[1], OWN * centre[2]]
-        lanes = lax.broadcasted_iota(jnp.int32, (height, LANES), 1)
+        lanes = lax.broadcasted_iota(jnp.int32, centre[0].shape, 1)
         sum_z = []
         for c in range(3):
-            end = pltpu.roll(sides[stage, c, pl.ds(start, height)], shift, 1)
+            end = pltpu.roll(take(sides, (stage, c), rows if outside else 0, 0, mode), shift, 1)
             up = jnp.where(lanes == LANES - 1, end, turn(mine[c] + tilt[c], -1))
             down = jnp.where(lanes == 0, end, turn(mine[c] - tilt[c], 1))
             sum_z.append(up + down)
@@ -582,19 +609,19 @@
             (x_up[2] + x_down[2]) + (y_up[2] + y_down[2]) + sum_z[2],
         ]
 
-    def sweep(source, target, low, high, stage):
-        def one(p, carry):
-            beside = neighbours(source, p, p - HALO, stage)
-            share = base[3, at(p)]
+    def sweep(source, target, low, high, stage, mode="wide"):
+        for x in range(low, high):
+            p = x + HALO
+            beside = neighbours(source, p, x, stage, mode)
+            share = take(base, (3,), p * rows, 0, mode)
             for c in range(3):
-                target[c, at(p)] = KEEP * source[c, at(p)] + base[c, at(p)] + share * beside[c]
-            return carry
-
-        by_two(low, high, one, 0)
+                kept = KEEP * take(source, (c,), p * rows, 0, mode)
+                fresh = kept + take(base, (c,), p * rows, 0, mode) + share * beside[c]
+                put(target, (c,), p * rows, mode, fresh)
 
     def residual(field, x, stage):
         p = x + HALO
-        beside = neighbours(field, p, x, stage, True)
+        beside = neighbours(field, p, x, stage, "own")
         g = stiff[own_rows(x)]
         heavy = g * DIAGONAL + MASS_TERM
         return [
@@ -602,17 +629,19 @@
         ]
 
     wait_halo((0,), halo_sem.at[0])
+    unpack_edges(0)
+    edge_sweep(edge_base, edge_a, 0)
+    edge_stage(edge_a, 1, False)
     greeted = min(1, len(rounds) - 1)
     for number in range(greeted):
         hear(number)
         hello(number + 1)
-    unpack(0)
-    edge_sweep(edge_base, edge_a, 0)
-    edge_stage(edge_a, 1, False)
-    sweep(base, field_b, HALO - 1, HALO + ex + 1, 0)
+    wait_halo((1,), halo_sem.at[1])
+    unpack_main(0)
+    sweep(base, field_a, -1, ex + 1, 0)
 
     def restrict(x, carry):
-        left = residual(field_b, x, 1)
+        left = residual(field_a, x, 1)
         return tuple(carry[c] + left[c] for c in range(3))
 
     sums = by_two(0, ex, restrict, (jnp.zeros((ey, LANES), jnp.float32),) * 3)
@@ -645,13 +674,20 @@
     peers(lambda x, y, z, dz: coarse_copy(x, y, z, dz).start())
     coarse_recv[reach, me[0] * count_y + me[1]] = grouped[:4]
 
-    wait_halo((1,), halo_sem.at[1])
-    unpack(1)
+    sweep(field_a, field_b, 0, ex, 1, "own")
+    wait_halo((2,), halo_sem.at[2])
+    unpack_edges(1)
     edge_sweep(edge_base, edge_a, 0)
     edge_sweep(edge_a, edge_b, 1)
-    sweep(base, field_a, 1, wide_x - 1, 0)
-    sweep(field_a, field_b, 2, wide_x - 2, 1)
-    wait_halo((0, 1), halo_sem.at[2])
+    wait_halo((3,), halo_sem.at[3])
+    unpack_main(1)
+    for low, high in ((1 - HALO, -1), (ex + 1, ex + HALO - 1)):
+        sweep(base, field_a, low, high, 0)
+    sweep(base, field_a, -1, ex + 1, 0, "rim")
+    for low, high in ((-2, 0), (ex, ex + 2)):
+        sweep(field_a, field_b, low, high, 1)
+    sweep(field_a, field_b, 0, ex, 1, "rim")
+    wait_halo(range(4), halo_sem.at[4])
     coarse_wait()
 
     coarse_rows = -(-(count_y + 1) // 8) * 8
@@ -787,7 +823,7 @@
         return carry
 
     by_two(2, wide_x - 2, correct, 0)
-    sweep(field_b, field_a, 3, wide_x - 3, 1)
+    sweep(field_b, field_a, -1, ex + 1, 1)
 
     def squares(x, carry):
         left = residual(field_a, x, 2)
@@ -870,6 +906,7 @@
             vmem(3, 3, rows),
             vmem(3, 3, rows),
             vmem(3, 3, 2 * rows),
+            vmem(4, 3, rows),
             vmem(2, layers, ex),
             vmem(2, layers, ex),
             vmem(2, 2, near, 2),
@@ -893,7 +930,7 @@
             vmem(total, 1),
             vmem(4 * EDGE * LANES, 1),
             dma((2,)),
-            dma((3,)),
+            dma((5,)),
             dma((2,)),
             dma((2,)),
             pltpu.SemaphoreType.REGULAR((max(1, rounds), 2)),

time: 27.4 us -> 26 us (0.949)
  Pallas kernels: 25.4 us -> 24 us
    pallas_call x1, Pallas kernels: 25.4 us -> 24 us  [on_device(): pl.pallas_call(functools.partial(kernel, counts, (ex, ey, ez)), out_shape...]
where the time goes in v4:
time: 26 us; the launch traced here: 25.9 us
  Pallas kernels  24 us (92%)
  local copies, waits for them, and re-layouts  1.26 us (5%)
  between operations  0.64 us (2%)
    pallas_call x1, Pallas kernels, on_device(): pl.pallas_call(functools.partial(kernel, counts, (ex, ey, ez)), out_shape...  24 us
    unnamed x1, local copies, waits for them, and re-layouts  0.75 us

profile of v4, /device:TPU:0, one launch (start us, length us, event | category | flops | bytes accessed | tf_op | source)
XLA Modules:
  0.0 25.9 jit_solution(2593947384444059022)
XLA Ops:
  0.6 24.0 %shard_map.41 = (f32[3,16,16,128]{3,2,1,0:T(8,128)S(1)}, f32[1,128]{1,0:T(1,128)S(1)}) custom-call(f32[3,16,16,128]{3,2,1,0:T(8,128)} %load_ref.1, s32[16,16,128]{2,1,0:T(8,128)} %damage_ref.1), custom_call_target="tpu_custom_call" | custom-call | tf_op jit(solution)/shard_map/pallas_call | solution.py:887
  24.6 0.7 %copy.5 = f32[3,16,16,128]{3,2,1,0:T(8,128)} copy(f32[3,16,16,128]{3,2,1,0:T(8,128)S(1)} %get-tuple-element.6) | data formatting | bytes 786432
  25.4 0.5 %slice_bitcast_fusion = f32[2]{0:T(128)} fusion(f32[1,128]{1,0:T(1,128)S(1)} %get-tuple-element.5), kind=kLoop, calls=%fused_computation | loop fusion | bytes 16 | tf_op jit(solution)/shard_map/squeeze | solution.py:940

commit v5 on v4

--- a/solution.py
+++ b/solution.py
@@ -82,6 +82,7 @@
     edge_b,
     sides,
     swung,
+    relay,
     y_send,
     y_recv,
     xyn_send,
@@ -315,8 +316,48 @@
             out.append((xy_send.at[xs, ys], xy_recv.at[1 - xs, 1 - ys], HALO * len(LAYERS)))
         return out
 
+    odd = lax.rem(me[1], 2) == 1
+    relayed = {
+        1: odd & (me[1] + 2 < count_y),
+        -1: jnp.logical_not(odd) & (me[1] >= 2),
+    }
+    relaying = {
+        1: jnp.logical_not(odd) & (me[1] + 2 < count_y),
+        -1: odd & (me[1] >= 3),
+    }
+
+    def far_copy(src, ys, device_y, final):
+        return pltpu.make_async_remote_copy(
+            src_ref=src,
+            dst_ref=y_recv.at[1 - ys, pl.ds(len(NEAR), len(FAR))] if final else relay,
+            send_sem=halo_sem.at[5 if final else 4],
+            recv_sem=halo_sem.at[3 if final else 6],
+            device_id=(me[0], device_y, me[2]),
+            device_id_type=MESH,
+        )
+
+    def send_to_relay():
+        for dy in (-1, 1):
+            ys = (dy + 1) // 2
+
+            @pl.when(relayed[dy])
+            def _():
+                far_copy(y_send.at[ys, pl.ds(len(NEAR), len(FAR))], ys, me[1] + 2 * dy, False).start()
+
+    def pass_on():
+        for dy in (-1, 1):
+
+            @pl.when(relaying[dy])
+            def _():
+                wait_bytes(len(FAR) * ex, halo_sem.at[6])
+                far_copy(relay, (1 - dy) // 2, me[1] + dy, True).start()
+
+    def finish_relay():
+        @pl.when(relaying[-1] | relaying[1])
+        def _():
+            wait_bytes(len(FAR) * ex, halo_sem.at[5])
+
     def start_sends(phase):
-        odd = lax.rem(me[1], 2) == 1
         ordered = []
         for turn_number in range(2):
             for number, d in enumerate(DIRECTIONS):
@@ -327,8 +368,13 @@
             parts = pieces(d, phase)
             if not parts:
                 continue
-
-            @pl.when(exists(*d) if condition is None else exists(*d) & condition)
+            here = exists(*d)
+            if condition is not None:
+                here = here & condition
+            if phase == 3 and d[0] == 0:
+                here = here & jnp.logical_not(relayed[d[1]])
+
+            @pl.when(here)
             def _():
                 for src, dst, _ in parts:
                     pltpu.make_async_remote_copy(
@@ -340,8 +386,9 @@
                         device_id_type=MESH,
                     ).start()
 
-    for phase in range(4):
-        start_sends(phase)
+    start_sends(0)
+    start_sends(1)
+    send_to_relay()
 
     def wait_bytes(size, sem):
         span = amount.at[pl.ds(0, size)]
@@ -636,6 +683,9 @@
     for number in range(greeted):
         hear(number)
         hello(number + 1)
+    pass_on()
+    start_sends(2)
+    start_sends(3)
     wait_halo((1,), halo_sem.at[1])
     unpack_main(0)
     sweep(base, field_a, -1, ex + 1, 0)
@@ -688,6 +738,7 @@
         sweep(field_a, field_b, low, high, 1)
     sweep(field_a, field_b, 0, ex, 1, "rim")
     wait_halo(range(4), halo_sem.at[4])
+    finish_relay()
     coarse_wait()
 
     coarse_rows = -(-(count_y + 1) // 8) * 8
@@ -907,6 +958,7 @@
             vmem(3, 3, rows),
             vmem(3, 3, 2 * rows),
             vmem(4, 3, rows),
+            vmem(len(FAR), ex),
             vmem(2, layers, ex),
             vmem(2, layers, ex),
             vmem(2, 2, near, 2),
@@ -930,7 +982,7 @@
             vmem(total, 1),
             vmem(4 * EDGE * LANES, 1),
             dma((2,)),
-            dma((5,)),
+            dma((7,)),
             dma((2,)),
             dma((2,)),
             pltpu.SemaphoreType.REGULAR((max(1, rounds), 2)),

time: 26 us -> 25.4 us (0.977)
  Pallas kernels: 24 us -> 23.3 us
    pallas_call x1, Pallas kernels: 24 us -> 23.3 us  [on_device(): pl.pallas_call(functools.partial(kernel, counts, (ex, ey, ez)), out_shape...]
where the time goes in v5:
time: 25.4 us; the launch traced here: 25.2 us
  Pallas kernels  23.3 us (92%)
  local copies, waits for them, and re-layouts  1.26 us (5%)
  between operations  0.64 us (3%)
    pallas_call x1, Pallas kernels, on_device(): pl.pallas_call(functools.partial(kernel, counts, (ex, ey, ez)), out_shape...  23.3 us
    unnamed x1, local copies, waits for them, and re-layouts  0.75 us
    squeeze x1, local copies, waits for them, and re-layouts, on_device(): return (displacement, norms[0, :2])  0.51 us

profile of v5, /device:TPU:0, one launch (start us, length us, event | category | flops | bytes accessed | tf_op | source)
XLA Modules:
  0.0 25.2 jit_solution(6287958159577461542)
XLA Ops:
  0.6 23.3 %shard_map.41 = (f32[3,16,16,128]{3,2,1,0:T(8,128)S(1)}, f32[1,128]{1,0:T(1,128)S(1)}) custom-call(f32[3,16,16,128]{3,2,1,0:T(8,128)} %load_ref.1, s32[16,16,128]{2,1,0:T(8,128)} %damage_ref.1), custom_call_target="tpu_custom_call" | custom-call | tf_op jit(solution)/shard_map/pallas_call | solution.py:938
  24.0 0.7 %copy.5 = f32[3,16,16,128]{3,2,1,0:T(8,128)} copy(f32[3,16,16,128]{3,2,1,0:T(8,128)S(1)} %get-tuple-element.6) | data formatting | bytes 786432
  24.7 0.5 %slice_bitcast_fusion = f32[2]{0:T(128)} fusion(f32[1,128]{1,0:T(1,128)S(1)} %get-tuple-element.5), kind=kLoop, calls=%fused_computation | loop fusion | bytes 16 | tf_op jit(solution)/shard_map/squeeze | solution.py:992

commit v6 on v5

--- a/solution.py
+++ b/solution.py
@@ -23,7 +23,6 @@
 LANES = 128
 YPAD = 8
 MESH = pl.DeviceIdType.MESH
-EXACT = lax.Precision.HIGHEST
 NEAR = ((0, 1), (1, 1), (2, 1), (3, 1), (0, 2), (1, 2), (2, 2))
 FAR = ((3, 2), (0, 3), (1, 3), (2, 3), (3, 3), (0, 4), (1, 4), (2, 4))
 LAYERS = NEAR + FAR
@@ -222,6 +221,17 @@
 
     zero = jnp.zeros((8, LANES), jnp.float32)
 
+    def pick(values, chosen):
+        parts, rest = [], values
+        for _ in range(3):
+            part = rest.astype(jnp.bfloat16).astype(jnp.float32)
+            parts.append(part)
+            rest = rest - part
+        joined = jnp.concatenate(parts, axis=0).astype(jnp.bfloat16)
+        out = jnp.dot(joined, chosen.astype(jnp.bfloat16), preferred_element_type=jnp.float32)
+        height = values.shape[0]
+        return out[:height] + out[height : 2 * height] + out[2 * height :]
+
     harm_copy.wait()
     load_copy.wait()
 
@@ -265,20 +275,24 @@
         for phase in range(2):
             qy_send[phase, xs, 0] = joined[2 * phase : 2 * phase + 2]
             qy_send[phase, xs, 1] = joined[ey - 2 - 2 * phase : ey - 2 * phase]
-    for side in range(2):
-        for i, (f, layer) in enumerate(LAYERS):
-            start = HALO * rows + ypad + (layer - 1 if side == 0 else ey - layer)
-            for half in range(ex // 8):
-                y_send[side, i, pl.ds(8 * half, 8)] = base[
-                    f, pl.ds(start + 8 * half * rows, 8, stride=rows)
-                ]
-            for xs in range(2):
-                x0 = 0 if xs == 0 else ex - HALO
-                xy_send[xs, side, i] = base[f, pl.ds(start + x0 * rows, HALO, stride=rows)]
-                if i < len(NEAR):
-                    x0 = 0 if xs == 0 else ex - 2
-                    xyn_send[xs, side, i] = base[f, pl.ds(start + x0 * rows, 2, stride=rows)]
-
+    def pack_main(late):
+        for side in range(2):
+            for i, (f, layer) in enumerate(LAYERS):
+                start = HALO * rows + ypad + (layer - 1 if side == 0 else ey - layer)
+                if (i >= len(NEAR)) == late:
+                    for half in range(ex // 8):
+                        y_send[side, i, pl.ds(8 * half, 8)] = base[
+                            f, pl.ds(start + 8 * half * rows, 8, stride=rows)
+                        ]
+                for xs in range(2):
+                    if late:
+                        x0 = 0 if xs == 0 else ex - HALO
+                        xy_send[xs, side, i] = base[f, pl.ds(start + x0 * rows, HALO, stride=rows)]
+                    elif i < len(NEAR):
+                        x0 = 0 if xs == 0 else ex - 2
+                        xyn_send[xs, side, i] = base[f, pl.ds(start + x0 * rows, 2, stride=rows)]
+
+    pack_main(False)
     pl.semaphore_wait(barrier, levels * count_x * count_y - 1)
 
     def pieces(d, phase):
@@ -357,7 +371,9 @@
         def _():
             wait_bytes(len(FAR) * ex, halo_sem.at[5])
 
-    def start_sends(phase):
+    one_sided = (me[1] == 0) | (me[1] == count_y - 1)
+
+    def start_sends(phase, only=None):
         ordered = []
         for turn_number in range(2):
             for number, d in enumerate(DIRECTIONS):
@@ -368,7 +384,7 @@
             parts = pieces(d, phase)
             if not parts:
                 continue
-            here = exists(*d)
+            here = exists(*d) if only is None else exists(*d) & only
             if condition is not None:
                 here = here & condition
             if phase == 3 and d[0] == 0:
@@ -388,7 +404,10 @@
 
     start_sends(0)
     start_sends(1)
+    pack_main(True)
     send_to_relay()
+    start_sends(2, one_sided)
+    start_sends(3, one_sided)
 
     def wait_bytes(size, sem):
         span = amount.at[pl.ds(0, size)]
@@ -684,8 +703,8 @@
         hear(number)
         hello(number + 1)
     pass_on()
-    start_sends(2)
-    start_sends(3)
+    start_sends(2, jnp.logical_not(one_sided))
+    start_sends(3, jnp.logical_not(one_sided))
     wait_halo((1,), halo_sem.at[1])
     unpack_main(0)
     sweep(base, field_a, -1, ex + 1, 0)
@@ -700,7 +719,7 @@
     source_lane = lax.broadcasted_iota(jnp.int32, (LANES, LANES), 0)
     target_lane = lax.broadcasted_iota(jnp.int32, (LANES, LANES), 1)
     gather = (source_lane // BLOCK == lax.rem(target_lane, cz)).astype(jnp.float32)
-    grouped = jnp.dot(stacked, gather, precision=EXACT, preferred_element_type=jnp.float32)
+    grouped = pick(stacked, gather)
     coarse_send[...] = grouped[:4]
 
     def coarse_copy(x, y, z, dz):
@@ -823,7 +842,7 @@
         jnp.where(target_lane < LANES // 2, pick_low, pick_high),
     )
     widen = jnp.concatenate([(source_lane == pick).astype(jnp.float32) for pick in picks], axis=1)
-    wide_all = jnp.dot(stack_w[...], widen, precision=EXACT, preferred_element_type=jnp.float32)
+    wide_all = pick(stack_w[...], widen)
 
     def drawn(xc, c, k):
         parts = []

time: 25.4 us -> 25.3 us (level)
  no operation moved by 1% of the time
where the time goes in v6:
time: 25.3 us; the launch traced here: 25.2 us
  Pallas kernels  23.3 us (92%)
  local copies, waits for them, and re-layouts  1.26 us (5%)
  between operations  0.64 us (3%)
    pallas_call x1, Pallas kernels, on_device(): pl.pallas_call(functools.partial(kernel, counts, (ex, ey, ez)), out_shape...  23.3 us
    unnamed x1, local copies, waits for them, and re-layouts  0.75 us
    squeeze x1, local copies, waits for them, and re-layouts, on_device(): return (displacement, norms[0, :2])  0.51 us

profile of v6, /device:TPU:0, one launch (start us, length us, event | category | flops | bytes accessed | tf_op | source)
XLA Modules:
  0.0 25.2 jit_solution(15422492403171414871)
XLA Ops:
  0.6 23.3 %shard_map.41 = (f32[3,16,16,128]{3,2,1,0:T(8,128)S(1)}, f32[1,128]{1,0:T(1,128)S(1)}) custom-call(f32[3,16,16,128]{3,2,1,0:T(8,128)} %load_ref.1, s32[16,16,128]{2,1,0:T(8,128)} %damage_ref.1), custom_call_target="tpu_custom_call" | custom-call | tf_op jit(solution)/shard_map/pallas_call | solution.py:957
  23.9 0.7 %copy.5 = f32[3,16,16,128]{3,2,1,0:T(8,128)} copy(f32[3,16,16,128]{3,2,1,0:T(8,128)S(1)} %get-tuple-element.6) | data formatting | bytes 786432
  24.7 0.5 %slice_bitcast_fusion = f32[2]{0:T(128)} fusion(f32[1,128]{1,0:T(1,128)S(1)} %get-tuple-element.5), kind=kLoop, calls=%fused_computation | loop fusion | bytes 16 | tf_op jit(solution)/shard_map/squeeze | solution.py:1011
